TPU v7x, 512 devices: a 4x2x32 block of a 4x8x32 slice. The times are simulated.
512 devices in a mesh: groups: 2 (over y), seq: 32 (over z), head: 4 (over x), rep: 2 (over core).
Axes of the slice: x: 4, y: 2, z: 32, core: 2. Of those that a mesh axis runs over, the one named last changes fastest.
The devices are a block of a 4x8x32 slice.
Arguments:
- tokens: bfloat16 [64, 4096], P('groups', ('seq', 'rep')), parts along dimension 0, may hold values from -6 to 6
- attn_gain: float32 [4096], P(('seq', 'rep')), may hold values from 0.25 to 1.75
- ffn_gain: float32 [4096], P(('seq', 'rep')), may hold values from 0.25 to 1.75
- w_query: bfloat16 [4096, 4096], P(('seq', 'rep'), 'head'), may hold values from -0.0625 to 0.0625
- w_key: bfloat16 [4096, 1024], P(('seq', 'rep'), 'head'), may hold values from -0.09375 to 0.09375
- w_value: bfloat16 [4096, 1024], P(('seq', 'rep'), 'head'), may hold values from -0.25 to 0.25
- w_out: bfloat16 [4096, 4096], P('head', ('seq', 'rep')), may hold values from -0.09375 to 0.09375
- w_gate: bfloat16 [4096, 7168], P(('seq', 'rep'), 'head'), may hold values from -0.09375 to 0.09375
- w_up: bfloat16 [4096, 7168], P(('seq', 'rep'), 'head'), may hold values from -0.09375 to 0.09375
- w_down: bfloat16 [7168, 4096], P('head', ('seq', 'rep')), may hold values from -0.0625 to 0.0625
- kv_pool: bfloat16 [2, 64, 32, 128, 1024], P(None, ('groups', 'seq'), 'head', 'rep'), parts along dimension 1, may hold values from -15 to 15
- lengths: int32 [64], P('groups'), parts along dimension 0, may hold values from 1 to 4096, 65536 in all
- pool_row: int32 [64], P('groups'), parts along dimension 0, may hold values from 0 to 31, each once
- block_table: int32 [64, 32], P('groups'), parts along dimension 0, may hold values from 0 to 31, each once within a row
Outputs:
- layer_out: bfloat16 [64, 4096], P('groups', ('seq', 'rep')), parts along dimension 0
- kv_decode: bfloat16 [2, 64, 4096, 1024], P(None, 'groups', ('seq', 'rep'), 'head'), parts along dimension 1
There are 2 independent parts, one for each index of `groups`. A program takes and returns all parts, laid end to end along the dimension named above; an argument that names none is the same for every part. Nothing has to cross between parts.
Inputs may be any that keep to these rules, and one draw needn't show every extreme that they name: One sequence reaches 4096; the lengths sum to 65536. `pool_row`: a permutation of the pool rows. `block_table`: every row is a permutation of the 32 slots.
All inputs are finite; a program needn't handle non-finite values.
Results may differ from a plain program's by a relative error of at most 0.008.
Values may be sent and summed in bfloat16 or wider, within the bound.
A program may use at most 64 MiB of HBM per device.

v0:
```python
import math

import jax
import jax.numpy as jnp
from jax import lax
from jax.sharding import PartitionSpec as P

D = 4096
H = 32
KVH = 8
HD = 128
BLK = 128


EPSILON = 1e-05
ROPE_LOG = math.log(500000.0)
FLOOR_SCORE = -1e30


def by_axis(value, axes):
    for axis in axes:
        value = lax.psum(value, axis)
    return value


def split_up(value, dim, peers):
    before, after = (value.shape[:dim], value.shape[dim + 1 :])
    return jnp.moveaxis(value.reshape(*before, peers, -1, *after), dim, 0)


def summed_on_arrival(value, axis, dim):
    tiles = split_up(value, dim, lax.axis_size(axis))
    arrived = lax.all_to_all(tiles, axis, split_axis=0, concat_axis=0, tiled=True)
    return arrived.sum(axis=0)


def sum_in_two_steps(value, axes, dim):
    far, near = axes
    tiles = split_up(value, dim, lax.axis_size(far))
    nearer = summed_on_arrival(tiles, near, dim + 1)
    arrived = lax.all_to_all(nearer, far, split_axis=0, concat_axis=0, tiled=True)
    return arrived.sum(axis=0)


def padded_to(lines, peers):
    spare = -len(lines) % peers
    return jnp.pad(lines, [(0, spare)] + [(0, 0)] * (lines.ndim - 1))


def from_everyone(value, axis):
    peers = lax.axis_size(axis)
    return lax.all_to_all(
        jnp.broadcast_to(value[None], (peers, *value.shape)), axis, 0, 0, tiled=True
    )


def joined_along(tiles, dim):
    dims = list(tiles.shape[1:])
    dims[dim] *= tiles.shape[0]
    return jnp.moveaxis(tiles, 0, dim).reshape(dims)


def whole_of(value, axes, dim):
    far, near = axes
    tiles = from_everyone(from_everyone(value, far), near)
    return joined_along(tiles.swapaxes(0, 1).reshape(-1, *value.shape), dim)


def total_of(value, axes):
    own = sum_in_two_steps(
        padded_to(value, lax.axis_size(axes[0]) * lax.axis_size(axes[1])), axes, 0
    )
    whole = whole_of(own, axes, 0)
    return whole[: len(value)].reshape(value.shape)


def together(arrays, axis):
    vector, at, finished = (jnp.concatenate([a.reshape(-1) for a in arrays]), 0, [])
    total = total_of(vector, axis)
    for a in arrays:
        finished.append(total[at : at + a.size].reshape(a.shape))
        at += a.size
    return tuple(finished)


def sent_together(arrays, axis, dim, along):
    widths = [a.shape[along] for a in arrays]
    both = jnp.concatenate(arrays, axis=along)
    filled = lax.all_gather(both, axis, axis=dim, tiled=True)
    return tuple(jnp.split(filled, [sum(widths[:k]) for k in range(1, len(widths))], axis=along))


def collected_together(value, axis):
    leaves = jax.tree.leaves(value)
    turns = sorted(range(len(leaves)), key=lambda k: -leaves[k].size)
    width = (1, *leaves[turns[0]].shape)[-1]
    lines = [
        jnp.pad(leaves[k].reshape(-1), (0, -leaves[k].size % width)).reshape(-1, width)
        for k in turns
    ]
    both, at, found = (from_everyone(jnp.concatenate(lines), axis), 0, {})
    for k, line in zip(turns, lines):
        section = both[:, at : at + len(line)].reshape(len(both), -1)
        found[k] = section[:, : leaves[k].size].reshape(-1, *leaves[k].shape)
        at += len(line)
    numbers = iter(range(len(leaves)))
    return jax.tree.map(lambda _: found[next(numbers)], value)


def combined_pairwise(pieces, combine):
    while len(jax.tree.leaves(pieces)[0]) > 1:
        pieces = jax.vmap(combine)(
            *(jax.tree.map(lambda part: part[side::2], pieces) for side in (0, 1))
        )
    return jax.tree.map(lambda part: part[0], pieces)


def merged_2(value, axis, combine):
    pieces = collected_together(value, axis)
    return combined_pairwise(pieces, combine)


def gather_directly(value, axis, dim):
    tiles = from_everyone(value, axis)
    return joined_along(tiles, dim)


def taken_together(value, axis):
    return from_everyone(value, axis).sum(axis=0)


def rotate(values, positions):
    half_dim = values.shape[-1] // 2
    freq_table = jnp.exp(
        jnp.arange(half_dim, dtype=jnp.float32) * (-2.0 * ROPE_LOG / values.shape[-1])
    )
    angles = positions[:, None, None] * freq_table
    cosine = jnp.cos(angles)
    sine_part = jnp.sin(angles)
    first_half = values[..., :half_dim]
    second_half = values[..., half_dim:]
    return jnp.concatenate(
        [
            first_half * cosine - second_half * sine_part,
            second_half * cosine + first_half * sine_part,
        ],
        axis=-1,
    )


def combine(first, second):
    top_a, mass_a, summed_a = first
    top_b, mass_b, summed_b = second
    largest = jnp.maximum(top_a, top_b)
    scale_a = jnp.exp(top_a - largest)
    scale_b = jnp.exp(top_b - largest)
    return (
        largest,
        mass_a * scale_a + mass_b * scale_b,
        summed_a * scale_a[..., None] + summed_b * scale_b[..., None],
    )


def partial_attention(queries, key_rows, value_rows, usable):
    factor = 1.0 / math.sqrt(queries.shape[-1])
    scores = (
        jnp.einsum("sngd,stnd->sngt", queries, key_rows, preferred_element_type=jnp.float32)
        * factor
    )
    scores = jnp.where(usable[:, None, None, :], scores, FLOOR_SCORE)
    highest = jnp.max(scores, axis=-1)
    weights = jnp.where(usable[:, None, None, :], jnp.exp(scores - highest[..., None]), 0.0)
    totals = jnp.sum(weights, axis=-1)
    summed = jnp.einsum(
        "sngt,stnd->sngd",
        weights.astype(jnp.bfloat16),
        value_rows,
        preferred_element_type=jnp.float32,
    )
    return (highest, totals, summed)


def finish(merged, queries, key_own, value_own):
    highest, totals, summed = merged
    factor = 1.0 / math.sqrt(queries.shape[-1])
    own_score = (
        jnp.sum(queries.astype(jnp.float32) * key_own.astype(jnp.float32)[:, :, None, :], axis=-1)
        * factor
    )
    largest = jnp.maximum(highest, own_score)
    kept_scale = jnp.exp(highest - largest)
    new_scale = jnp.exp(own_score - largest)
    denominator = totals * kept_scale + new_scale
    mixed = (
        summed * kept_scale[..., None]
        + new_scale[..., None] * value_own.astype(jnp.float32)[:, :, None, :]
    )
    return mixed / denominator[..., None]


def shards(
    tokens,
    attn_gain,
    ffn_gain,
    w_query,
    w_key,
    w_value,
    w_out,
    w_gate,
    w_up,
    w_down,
    kv_pool,
    lengths,
    pool_row,
    block_table,
):
    seq_count = tokens.shape[0]
    per_group = H // KVH
    kv_local = w_key.shape[1] // HD
    residual = tokens.astype(jnp.float32)
    square_sum = by_axis(jnp.sum(residual * residual, axis=1), ("seq", "rep"))
    normed = (residual * lax.rsqrt(square_sum / D + EPSILON)[:, None] * attn_gain).astype(
        jnp.bfloat16
    )
    queries, keys_new, values_new = together(
        (
            jnp.dot(normed, w_query, preferred_element_type=jnp.float32),
            jnp.dot(normed, w_key, preferred_element_type=jnp.float32),
            jnp.dot(normed, w_value, preferred_element_type=jnp.float32),
        ),
        ("seq", "rep"),
    )
    positions = lengths.astype(jnp.float32)
    rot_queries = rotate(queries.reshape(seq_count, -1, HD), positions).astype(jnp.bfloat16)
    rot_keys = rotate(keys_new.reshape(seq_count, kv_local, HD), positions).astype(jnp.bfloat16)
    new_values = values_new.reshape(seq_count, kv_local, HD).astype(jnp.bfloat16)
    slot_count = kv_pool.shape[2]
    half_rows = kv_pool.shape[3]
    row_here = lax.axis_index("seq")
    head_here = lax.axis_index("head")
    rep_here = lax.axis_index("rep")
    seq_ids = jnp.arange(seq_count, dtype=jnp.int32)
    owner_seq = jnp.sum(jnp.where(pool_row == row_here, seq_ids, 0))
    table_row = lax.dynamic_index_in_dim(block_table, owner_seq, 0, keepdims=False)
    length_here = lax.dynamic_index_in_dim(lengths, owner_seq, 0, keepdims=False)
    block_count = table_row.shape[0]
    slot_ids = head_here * slot_count + jnp.arange(slot_count, dtype=jnp.int32)
    block_ids = jnp.arange(block_count, dtype=jnp.int32)
    block_of_slot = jnp.sum(
        jnp.where(table_row[None, :] == slot_ids[:, None], block_ids[None, :], 0), axis=1
    )
    token_pos = (
        block_of_slot[:, None] * BLK
        + rep_here * half_rows
        + jnp.arange(half_rows, dtype=jnp.int32)[None, :]
    )
    is_live = token_pos < length_here
    pool_local = kv_pool[:, 0]
    cleaned = jnp.where(is_live[None, :, :, None], pool_local, jnp.zeros((), jnp.bfloat16))
    by_head = lax.all_to_all(cleaned, "head", split_axis=3, concat_axis=1, tiled=True)
    logical = jnp.take(by_head, table_row, axis=1)
    arrived = lax.all_to_all(logical[:, None], "seq", split_axis=2, concat_axis=1, tiled=True)
    by_row = arrived[:, :, 0]
    decoded = jnp.take(by_row, pool_row, axis=1)
    every_query, every_key, every_value = (
        lax.all_gather(rot_queries, "head", axis=1, tiled=True),
        *sent_together((rot_keys, new_values), "head", 1, 0),
    )
    query_row = lax.dynamic_index_in_dim(every_query, owner_seq, 0, keepdims=False).reshape(
        1, KVH, per_group, HD
    )
    key_row = lax.dynamic_index_in_dim(every_key, owner_seq, 0, keepdims=True)
    value_row = lax.dynamic_index_in_dim(every_value, owner_seq, 0, keepdims=True)
    key_rows = cleaned[0].reshape(1, slot_count * half_rows, KVH, HD)
    value_rows = cleaned[1].reshape(1, slot_count * half_rows, KVH, HD)
    usable = is_live.reshape(1, slot_count * half_rows)
    merged = merged_2(
        partial_attention(query_row, key_rows, value_rows, usable), ("head", "rep"), combine
    )
    mixed = finish(merged, query_row, key_row, value_row).reshape(-1)
    head_width = kv_local * per_group * HD
    my_heads = lax.dynamic_slice_in_dim(mixed, head_here * head_width, head_width, 0).astype(
        jnp.bfloat16
    )
    gathered = gather_directly(my_heads[None, :], "seq", 0)
    attn_heads = jnp.take(gathered, pool_row, axis=0)
    attn_proj = taken_together(
        jnp.dot(attn_heads, w_out, preferred_element_type=jnp.float32), "head"
    )
    middle = residual + attn_proj
    square_mid = by_axis(jnp.sum(middle * middle, axis=1), ("seq", "rep"))
    normed_mid = (middle * lax.rsqrt(square_mid / D + EPSILON)[:, None] * ffn_gain).astype(
        jnp.bfloat16
    )
    gate_sum, up_sum = together(
        (
            jnp.dot(normed_mid, w_gate, preferred_element_type=jnp.float32),
            jnp.dot(normed_mid, w_up, preferred_element_type=jnp.float32),
        ),
        ("seq", "rep"),
    )
    hidden = (jax.nn.silu(gate_sum) * up_sum).astype(jnp.bfloat16)
    down_part = taken_together(jnp.dot(hidden, w_down, preferred_element_type=jnp.float32), "head")
    return ((middle + down_part).astype(jnp.bfloat16), decoded)


def solution(mesh):
    in_specs = (
        P("groups", ("seq", "rep")),
        P(("seq", "rep")),
        P(("seq", "rep")),
        P(("seq", "rep"), "head"),
        P(("seq", "rep"), "head"),
        P(("seq", "rep"), "head"),
        P("head", ("seq", "rep")),
        P(("seq", "rep"), "head"),
        P(("seq", "rep"), "head"),
        P("head", ("seq", "rep")),
        P(None, ("groups", "seq"), "head", "rep", None),
        P("groups"),
        P("groups"),
        P("groups", None),
    )
    out_specs = (P("groups", ("seq", "rep")), P(None, "groups", ("seq", "rep"), "head"))
    return jax.shard_map(shards, mesh=mesh, in_specs=in_specs, out_specs=out_specs, check_vma=False)
```

profile of v0, /device:TPU:33, one launch (start us, length us, event | category | flops | bytes accessed | tf_op | source)
XLA Modules:
  0.0 662.0 jit_solution(13865352944451561582)
XLA Ops:
  1.6 83.0 %psum.28 = f32[32]{0:T(128)S(1)} all-reduce(f32[32]{0:T(128)S(1)} %fusion.13), channel_id=1, replica_groups=mesh['groups'=2,'seq'=32,'head'=4,'rep'=2] {'seq'}, use_global_device_ids=true, to_apply=%region_3.4 | all-reduce | flops 32 | bytes 256 | tf_op jit(solution)/shard_map/psum | solution.py:22
  84.6 16.8 %psum.29 = f32[32]{0:T(128)S(1)} all-reduce(f32[32]{0:T(128)S(1)} %psum.28), channel_id=1, replica_groups=mesh['groups'=2,'seq'=32,'head'=4,'rep'=2] {'rep'}, use_global_device_ids=true, to_apply=%region_4.5 | all-reduce | flops 32 | bytes 256 | tf_op jit(solution)/shard_map/psum | solution.py:22
  109.4 5.0 all-to-all-start.1
  124.1 16.6 %all-to-all-done.1 = f32[32,1,768]{2,1,0:T(1,128)S(1)} async-done(((f32[32,1,768]{2,1,0:T(1,128)}), f32[32,1,768]{2,1,0:T(1,128)S(1)}, u32[]{:S(2)}, u32[]{:S(2)}) %all-to-all-start.1) | async-done | bytes 98336 | tf_op jit(solution)/shard_map/all_to_all | solution.py:41
  160.1 10.4 %all-to-all-done.2 = f32[32,1,768]{2,1,0:T(1,128)S(1)} async-done(((f32[32,1,768]{2,1,0:T(1,128)}), f32[32,1,768]{2,1,0:T(1,128)S(1)}, u32[]{:S(2)}, u32[]{:S(2)}) %all-to-all-start.2) | async-done | bytes 98336 | tf_op jit(solution)/shard_map/all_to_all | solution.py:52
  170.6 8.3 %all_to_all.98 = f32[2,32,768]{2,1,0:T(8,128)S(1)} all-to-all(f32[2,32,768]{2,1,0:T(8,128)S(1)} %broadcast_in_dim.93), channel_id=1, replica_groups=mesh['groups'=2,'seq'=32,'head'=4,'rep'=2] {'rep'}, dimensions={0} | all-to-all | bytes 393216 | tf_op jit(solution)/shard_map/all_to_all | solution.py:52
  179.8 9.8 %all_gather.7 = bf16[64,8,128]{2,0,1:T(8,128)(2,1)S(1)} all-gather(bf16[64,2,128]{2,0,1:T(8,128)(2,1)S(1)} %copy.213), channel_id=1, replica_groups=mesh['groups'=2,'seq'=32,'head'=4,'rep'=2] {'head'}, dimensions={1}, use_global_device_ids=true | all-gather | bytes 163840 | tf_op jit(solution)/shard_map/all_gather | solution.py:89
  189.7 9.6 %all_gather.6 = bf16[32,32,128]{2,1,0:T(8,128)(2,1)S(1)} all-gather(bf16[32,8,128]{2,1,0:T(8,128)(2,1)S(1)} %pad_maximum_fusion.1), channel_id=1, replica_groups=mesh['groups'=2,'seq'=32,'head'=4,'rep'=2] {'head'}, dimensions={1}, use_global_device_ids=true | all-gather | bytes 327680 | tf_op jit(solution)/shard_map/all_gather | solution.py:266
  201.3 9.3 %all-to-all-start.4 = ((f32[8,34,128]{2,1,0:T(8,128)}), f32[8,34,128]{2,1,0:T(8,128)S(1)}, u32[]{:S(2)}, u32[]{:S(2)}) async-start(f32[8,34,128]{2,1,0:T(8,128)} %broadcast_in_dim.156), calls=%async_computation.4 | async-start | bytes 327680 | tf_op jit(solution)/shard_map/all_to_all | solution.py:52
  210.8 5.4 all-to-all-done.4
  221.0 9.2 %all-to-all-start.5 = ((bf16[32,2,512]{2,1,0:T(2,128)(2,1)}), bf16[32,2,512]{2,1,0:T(2,128)(2,1)S(1)}, u32[]{:S(2)}, u32[]{:S(2)}) async-start(bf16[32,2,512]{2,1,0:T(2,128)(2,1)} %reshape.425), calls=%async_computation.5 | async-start | bytes 131072 | tf_op jit(solution)/shard_map/all_to_all | solution.py:52
  230.2 22.9 %all-to-all-done.5 = bf16[32,2,512]{2,1,0:T(2,128)(2,1)S(1)} async-done(((bf16[32,2,512]{2,1,0:T(2,128)(2,1)}), bf16[32,2,512]{2,1,0:T(2,128)(2,1)S(1)}, u32[]{:S(2)}, u32[]{:S(2)}) %all-to-all-start.5) | async-done | bytes 65568 | tf_op jit(solution)/shard_map/all_to_all | solution.py:52
  254.2 6.7 %all_to_all.99 = f32[4,1,2048]{2,1,0:T(1,128)S(1)} all-to-all(f32[4,1,2048]{2,1,0:T(1,128)S(1)} %reshape.427), channel_id=1, replica_groups=mesh['groups'=2,'seq'=32,'head'=4,'rep'=2] {'head'}, dimensions={0} | all-to-all | bytes 65536 | tf_op jit(solution)/shard_map/all_to_all | solution.py:52
  262.3 39.7 %psum.30 = f32[32]{0:T(128)S(1)} all-reduce(f32[32]{0:T(128)S(1)} %multiply_reduce_fusion), channel_id=1, replica_groups=mesh['groups'=2,'seq'=32,'head'=4,'rep'=2] {'seq'}, use_global_device_ids=true, to_apply=%region_12.13 | all-reduce | flops 32 | bytes 256 | tf_op jit(solution)/shard_map/psum | solution.py:22
  302.1 20.1 %psum.31 = f32[32]{0:T(128)S(1)} all-reduce(f32[32]{0:T(128)S(1)} %psum.30), channel_id=1, replica_groups=mesh['groups'=2,'seq'=32,'head'=4,'rep'=2] {'rep'}, use_global_device_ids=true, to_apply=%region_13.14 | all-reduce | flops 32 | bytes 256 | tf_op jit(solution)/shard_map/psum | solution.py:22
  327.9 6.4 all-to-all-start.8
  338.7 5.9 reshape.431
  344.6 28.3 %all-to-all-done.8 = f32[32,1,1792]{2,1,0:T(1,128)S(1)} async-done(((f32[32,1,1792]{2,1,0:T(1,128)}), f32[32,1,1792]{2,1,0:T(1,128)S(1)}, u32[]{:S(2)}, u32[]{:S(2)}) %all-to-all-start.8) | async-done | bytes 229408 | tf_op jit(solution)/shard_map/all_to_all | solution.py:41
  376.7 24.7 %all-to-all-done.12 = bf16[4,2,131072]{2,1,0:T(2,128)(2,1)S(1)} async-done(((bf16[4,2,131072]{2,1,0:T(2,128)(2,1)}), bf16[4,2,131072]{2,1,0:T(2,128)(2,1)S(1)}, u32[]{:S(2)}, u32[]{:S(2)}) %all-to-all-start.12) | async-done | bytes 2097184 | tf_op jit(solution)/shard_map/all_to_all | solution.py:260
  411.0 5.2 copy.235
  420.2 21.9 %all-to-all-done.9 = f32[32,1,1792]{2,1,0:T(1,128)S(1)} async-done(((f32[32,1,1792]{2,1,0:T(1,128)}), f32[32,1,1792]{2,1,0:T(1,128)S(1)}, u32[]{:S(2)}, u32[]{:S(2)}) %all-to-all-start.9) | async-done | bytes 229408 | tf_op jit(solution)/shard_map/all_to_all | solution.py:52
  442.2 8.8 %all_to_all.101 = f32[2,32,1792]{2,1,0:T(8,128)S(1)} all-to-all(f32[2,32,1792]{2,1,0:T(8,128)S(1)} %broadcast_in_dim.163), channel_id=1, replica_groups=mesh['groups'=2,'seq'=32,'head'=4,'rep'=2] {'rep'}, dimensions={0} | all-to-all | bytes 917504 | tf_op jit(solution)/shard_map/all_to_all | solution.py:52
  460.2 4.9 all-to-all-start.13
  466.6 189.9 %all-to-all-done.13 = bf16[2,1,32,64,256]{4,3,0,1,2:T(8,128)(2,1)S(1)} async-done(((bf16[2,1,32,64,256]{4,3,0,1,2:T(8,128)(2,1)}), bf16[2,1,32,64,256]{4,3,0,1,2:T(8,128)(2,1)S(1)}, u32[]{:S(2)}, u32[]{:S(2)}) %all-to-all-start.13) | async-done | bytes 2097184 | tf_op jit(solution)/shard_map/all_to_all | solution.py:262
  (177 shorter events, 89.9 us)
Async XLA Ops:
  0.6 321.6 %copy-start = (bf16[64,1792]{1,0:T(8,128)(2,1)S(1)}, bf16[64,1792]{1,0:T(8,128)(2,1)}, u32[]{:S(2)}) copy-start(bf16[64,1792]{1,0:T(8,128)(2,1)} %param.24) | copy-start | bytes 688132
  0.6 113.8 %copy-start.6 = (s32[32]{0:T(128)S(1)}, s32[32]{0:T(128)}, u32[]{:S(2)}) copy-start(s32[32]{0:T(128)} %param.28) | copy-start | bytes 388
  0.7 115.7 %copy-start.2 = (bf16[2,1,8,64,1024]{4,3,2,1,0:T(8,128)(2,1)S(1)}, bf16[2,1,8,64,1024]{4,3,2,1,0:T(8,128)(2,1)}, u32[]{:S(2)}) copy-start(bf16[2,1,8,64,1024]{4,3,2,1,0:T(8,128)(2,1)} %param.26) | copy-start | bytes 6291460
  109.4 31.4 %all-to-all-start.1 = ((f32[32,1,768]{2,1,0:T(1,128)}), f32[32,1,768]{2,1,0:T(1,128)S(1)}, u32[]{:S(2)}, u32[]{:S(2)}) async-start(f32[32,1,768]{2,1,0:T(1,128)} %all_to_all.65), calls=%async_computation.1 | async-start | bytes 196608 | tf_op jit(solution)/shard_map/all_to_all | solution.py:41
  116.4 5.6 copy-start.9
  141.6 29.0 %all-to-all-start.2 = ((f32[32,1,768]{2,1,0:T(1,128)}), f32[32,1,768]{2,1,0:T(1,128)S(1)}, u32[]{:S(2)}, u32[]{:S(2)}) async-start(f32[32,1,768]{2,1,0:T(1,128)} %broadcast_in_dim.91), calls=%async_computation.2 | async-start | bytes 196608 | tf_op jit(solution)/shard_map/all_to_all | solution.py:52
  160.0 39.5 %copy-start.1 = (bf16[512,8,128]{0,2,1:T(8,128)(2,1)S(1)}, bf16[512,8,128]{0,2,1:T(8,128)(2,1)}, u32[]{:S(2)}) copy-start(bf16[512,8,128]{0,2,1:T(8,128)(2,1)} %reshape.423) | copy-start | bytes 3145732
  200.5 53.4 %copy-start.8 = (bf16[1024,64]{0,1:T(8,128)(2,1)S(1)}, bf16[1024,64]{0,1:T(8,128)(2,1)}, u32[]{:S(2)}) copy-start(bf16[1024,64]{0,1:T(8,128)(2,1)} %param.22) | copy-start | bytes 393220
  201.3 60.9 %copy-start.3 = (bf16[32,64]{1,0:T(8,128)(2,1)S(1)}, bf16[32,64]{1,0:T(8,128)(2,1)}, u32[]{:S(2)}) copy-start(bf16[32,64]{1,0:T(8,128)(2,1)} %param.16) | copy-start | bytes 12292
  201.3 120.9 %copy-start.5 = (f32[64]{0:T(128)S(1)}, f32[64]{0:T(128)}, u32[]{:S(2)}) copy-start(f32[64]{0:T(128)} %param.18) | copy-start | bytes 772
  201.3 14.9 %all-to-all-start.4 = ((f32[8,34,128]{2,1,0:T(8,128)}), f32[8,34,128]{2,1,0:T(8,128)S(1)}, u32[]{:S(2)}, u32[]{:S(2)}) async-start(f32[8,34,128]{2,1,0:T(8,128)} %broadcast_in_dim.156), calls=%async_computation.4 | async-start | bytes 327680 | tf_op jit(solution)/shard_map/all_to_all | solution.py:52
  218.2 104.3 %copy-start.4 = (bf16[64,1792]{1,0:T(8,128)(2,1)S(1)}, bf16[64,1792]{1,0:T(8,128)(2,1)}, u32[]{:S(2)}) copy-start(bf16[64,1792]{1,0:T(8,128)(2,1)} %param.23) | copy-start | bytes 688132
  221.0 32.1 %all-to-all-start.5 = ((bf16[32,2,512]{2,1,0:T(2,128)(2,1)}), bf16[32,2,512]{2,1,0:T(2,128)(2,1)S(1)}, u32[]{:S(2)}, u32[]{:S(2)}) async-start(bf16[32,2,512]{2,1,0:T(2,128)(2,1)} %reshape.425), calls=%async_computation.5 | async-start | bytes 131072 | tf_op jit(solution)/shard_map/all_to_all | solution.py:52
  327.9 45.0 %all-to-all-start.8 = ((f32[32,1,1792]{2,1,0:T(1,128)}), f32[32,1,1792]{2,1,0:T(1,128)S(1)}, u32[]{:S(2)}, u32[]{:S(2)}) async-start(f32[32,1,1792]{2,1,0:T(1,128)} %all_to_all.73), calls=%async_computation.8 | async-start | bytes 458752 | tf_op jit(solution)/shard_map/all_to_all | solution.py:41
  372.9 28.5 %all-to-all-start.12 = ((bf16[4,2,131072]{2,1,0:T(2,128)(2,1)}), bf16[4,2,131072]{2,1,0:T(2,128)(2,1)S(1)}, u32[]{:S(2)}, u32[]{:S(2)}) async-start(bf16[4,2,131072]{2,1,0:T(2,128)(2,1)} %reshape.431), calls=%async_computation.12 | async-start | bytes 4194304 | tf_op jit(solution)/shard_map/all_to_all | solution.py:260
  402.2 39.9 %all-to-all-start.9 = ((f32[32,1,1792]{2,1,0:T(1,128)}), f32[32,1,1792]{2,1,0:T(1,128)S(1)}, u32[]{:S(2)}, u32[]{:S(2)}) async-start(f32[32,1,1792]{2,1,0:T(1,128)} %broadcast_in_dim.161), calls=%async_computation.9 | async-start | bytes 458752 | tf_op jit(solution)/shard_map/all_to_all | solution.py:52
  442.1 9.6 %copy-start.7 = (bf16[1792,64]{0,1:T(8,128)(2,1)S(1)}, bf16[1792,64]{0,1:T(8,128)(2,1)}, u32[]{:S(2)}) copy-start(bf16[1792,64]{0,1:T(8,128)(2,1)} %param.25) | copy-start | bytes 688132
  452.7 7.6 %all-to-all-start.11 = ((f32[4,1,2048]{2,1,0:T(1,128)}), f32[4,1,2048]{2,1,0:T(1,128)S(1)}, u32[]{:S(2)}, u32[]{:S(2)}) async-start(f32[4,1,2048]{2,1,0:T(1,128)} %reshape.429), calls=%async_computation.11 | async-start | bytes 65536 | tf_op jit(solution)/shard_map/all_to_all | solution.py:52
  460.2 196.3 %all-to-all-start.13 = ((bf16[2,1,32,64,256]{4,3,0,1,2:T(8,128)(2,1)}), bf16[2,1,32,64,256]{4,3,0,1,2:T(8,128)(2,1)S(1)}, u32[]{:S(2)}, u32[]{:S(2)}) async-start(bf16[2,1,32,64,256]{4,3,0,1,2:T(8,128)(2,1)} %select_bitcast_fusion.1), calls=%async_computation.13 | async-start | bytes 4194304 | tf_op jit(solution)/shard_map/all_to_all | solution.py:262
where the time goes:
time: 669 us; the launch traced here: 662 us
  waiting for transfers between devices  323 us (48%)
  blocking collectives  211 us (32%)
  starting transfers between devices  51.6 us (8%)
  local copies, waits for them, and re-layouts  50.3 us (8%)
  other arithmetic  18.9 us (3%)
    all_to_all x1, waiting for transfers between devices, shards(): lax.all_to_all(logical[:, None], 'seq', split_axis=2, concat_axis=1, tile...  190 us
    psum x4, blocking collectives, by_axis(): value = lax.psum(value, axis)  160 us
    all_to_all x5, waiting for transfers between devices, from_everyone(): lax.all_to_all(jnp.broadcast_to(value[None], (peers, *value.shape)), axis...  63.2 us
    all_to_all x2, waiting for transfers between devices, sum_in_two_steps(): lax.all_to_all(nearer, far, split_axis=0, concat_axis=0, tiled=True)  44.9 us
    all_to_all x5, starting transfers between devices, from_everyone(): lax.all_to_all(jnp.broadcast_to(value[None], (peers, *value.shape)), axis...  31.5 us
    all_to_all x1, waiting for transfers between devices, shards(): lax.all_to_all(cleaned, 'head', split_axis=3, concat_axis=1, tiled=True)  24.7 us
    all_to_all x3, blocking collectives, from_everyone(): lax.all_to_all(jnp.broadcast_to(value[None], (peers, *value.shape)), axis...  23.8 us
    unnamed x42, local copies, waits for them, and re-layouts  18.8 us
  transfers between devices with their start and end apart: 9, of which 9 were waited for; matrix products, arithmetic and copies ran while one was open for 7% of the time, Pallas kernels for 0%

commit v1 on v0

v1 whole, which is shorter than its diff:
```python
import math

import jax
import jax.numpy as jnp
from jax import lax
from jax.sharding import PartitionSpec as P

D = 4096
H = 32
KVH = 8
HD = 128
BLK = 128
LANES = 128

EPSILON = 1e-05
ROPE_LOG = math.log(500000.0)
FLOOR_SCORE = -1e30


def exchanged(tiles, axis):
    return lax.all_to_all(tiles, axis, split_axis=0, concat_axis=0, tiled=True)


def from_everyone(value, axis):
    peers = lax.axis_size(axis)
    return exchanged(jnp.broadcast_to(value[None], (peers, *value.shape)), axis)


def rotate(values, position):
    half_dim = values.shape[-1] // 2
    freq_table = jnp.exp(
        jnp.arange(half_dim, dtype=jnp.float32) * (-2.0 * ROPE_LOG / values.shape[-1])
    )
    angles = position * freq_table
    cosine = jnp.cos(angles)
    sine_part = jnp.sin(angles)
    first_half = values[..., :half_dim]
    second_half = values[..., half_dim:]
    return jnp.concatenate(
        [
            first_half * cosine - second_half * sine_part,
            second_half * cosine + first_half * sine_part,
        ],
        axis=-1,
    )


def rows_to_owner(parts, squares, kind):
    rows = squares.shape[0]
    widths = [a.shape[2] for a in parts]
    extra = jnp.broadcast_to(squares[:, None, None], (rows, 2, LANES))
    tiles = jnp.concatenate([*parts, extra], axis=2).swapaxes(0, 1)
    pair = exchanged(tiles, "rep").sum(axis=0)
    width = sum(widths)
    sums, square = pair[:, :width], pair[:, width:]
    if kind != jnp.float32:
        lead = square.astype(kind)
        rest = (square - lead.astype(jnp.float32)).astype(kind)
        square = jnp.concatenate([lead, rest], axis=1)
        sums = sums.astype(kind)
    sent = jnp.concatenate([sums, square], axis=1)
    got = exchanged(sent[:, None, :], "seq")[:, 0].astype(jnp.float32).sum(axis=0)
    found, at = [], 0
    for w in widths:
        found.append(got[at : at + w])
        at += w
    total = got[at] if kind == jnp.float32 else got[at] + got[at + LANES]
    return found, total


def partial_attention(queries, key_rows, value_rows, usable):
    factor = 1.0 / math.sqrt(queries.shape[-1])
    scores = (
        jnp.einsum("ngd,tnd->ngt", queries, key_rows, preferred_element_type=jnp.float32) * factor
    )
    scores = jnp.where(usable[None, None, :], scores, FLOOR_SCORE)
    highest = jnp.max(scores, axis=-1)
    weights = jnp.where(usable[None, None, :], jnp.exp(scores - highest[..., None]), 0.0)
    totals = jnp.sum(weights, axis=-1)
    summed = jnp.einsum(
        "ngt,tnd->ngd",
        weights.astype(jnp.bfloat16),
        value_rows,
        preferred_element_type=jnp.float32,
    )
    return (highest, totals, summed)


def shards(
    tokens,
    attn_gain,
    ffn_gain,
    w_query,
    w_key,
    w_value,
    w_out,
    w_gate,
    w_up,
    w_down,
    kv_pool,
    lengths,
    pool_row,
    block_table,
):
    seq_count = tokens.shape[0]
    per_group = H // KVH
    slot_count = kv_pool.shape[2]
    half_rows = kv_pool.shape[3]
    row_here = lax.axis_index("seq")
    head_here = lax.axis_index("head")
    rep_here = lax.axis_index("rep")
    seq_ids = jnp.arange(seq_count, dtype=jnp.int32)
    to_row = pool_row[None, :] == seq_ids[:, None]
    owner_seq = jnp.sum(jnp.where(pool_row == row_here, seq_ids, 0))
    table_row = lax.dynamic_index_in_dim(block_table, owner_seq, 0, keepdims=False)
    length_here = lax.dynamic_index_in_dim(lengths, owner_seq, 0, keepdims=False)

    pool_local = kv_pool[:, 0]
    moved = []
    for side in range(2):
        by_head = lax.all_to_all(pool_local[side], "head", split_axis=2, concat_axis=0, tiled=True)
        logical = jnp.take(by_head, table_row, axis=0)
        moved.append(lax.all_to_all(logical, "seq", split_axis=0, concat_axis=0, tiled=True))
    here = row_here * BLK + rep_here * half_rows + jnp.arange(half_rows, dtype=jnp.int32)
    live_out = here[None, :] < lengths[:, None]
    decoded = jnp.stack(
        [
            jnp.where(live_out[:, :, None], jnp.take(m, pool_row, axis=0), jnp.zeros((), m.dtype))
            for m in moved
        ]
    )

    ordered = jnp.dot(
        to_row.astype(jnp.bfloat16), tokens, preferred_element_type=jnp.float32
    )
    residual = ordered
    squares = jnp.sum(residual * residual, axis=1)
    scaled = (residual * attn_gain).astype(jnp.bfloat16)
    (query, key_new, value_new), square_sum = rows_to_owner(
        [
            jnp.dot(scaled, w, preferred_element_type=jnp.float32).reshape(seq_count, 2, -1)
            for w in (w_query, w_key, w_value)
        ],
        squares,
        jnp.float32,
    )
    scale = lax.rsqrt(square_sum / D + EPSILON)
    position = length_here.astype(jnp.float32)
    query = rotate((query * scale).reshape(per_group, HD), position).astype(jnp.bfloat16)
    key_new = rotate((key_new * scale).reshape(1, HD), position).astype(jnp.bfloat16)
    value_new = (value_new * scale).reshape(1, HD).astype(jnp.bfloat16)
    every_query = from_everyone(query, ("head", "rep"))

    block_ids = jnp.arange(table_row.shape[0], dtype=jnp.int32)
    slot_ids = head_here * slot_count + jnp.arange(slot_count, dtype=jnp.int32)
    block_of_slot = jnp.sum(
        jnp.where(table_row[None, :] == slot_ids[:, None], block_ids[None, :], 0), axis=1
    )
    token_pos = (
        block_of_slot[:, None] * BLK
        + rep_here * half_rows
        + jnp.arange(half_rows, dtype=jnp.int32)[None, :]
    )
    usable = (token_pos < length_here).reshape(-1)
    highest, totals, summed = partial_attention(
        every_query,
        pool_local[0].reshape(-1, KVH, HD),
        pool_local[1].reshape(-1, KVH, HD),
        usable,
    )
    state = jnp.concatenate(
        [
            summed,
            jnp.broadcast_to(highest[..., None], summed.shape),
            jnp.broadcast_to(totals[..., None], summed.shape),
        ],
        axis=-1,
    )
    parts = exchanged(state, ("head", "rep"))
    tops, masses = parts[..., HD], parts[..., 2 * HD]
    factor = 1.0 / math.sqrt(HD)
    own_score = (
        jnp.sum(query.astype(jnp.float32) * key_new.astype(jnp.float32), axis=-1) * factor
    )
    largest = jnp.maximum(jnp.max(tops, axis=0), own_score)
    kept = jnp.exp(tops - largest[None])
    own = jnp.exp(own_score - largest)
    mass = jnp.sum(masses * kept, axis=0) + own
    mixed = (
        jnp.sum(parts[..., :HD] * kept[..., None], axis=0)
        + own[:, None] * value_new.astype(jnp.float32)
    ) / mass[:, None]
    attn = mixed.reshape(-1).astype(jnp.bfloat16)
    attn_half = from_everyone(attn, "seq")
    attn_rows = from_everyone(attn_half, "rep").swapaxes(0, 1).reshape(seq_count, -1)
    attn_proj = from_everyone(
        jnp.dot(attn_rows, w_out, preferred_element_type=jnp.float32), "head"
    ).sum(axis=0)
    middle = residual + attn_proj

    square_mid = jnp.sum(middle * middle, axis=1)
    scaled_mid = (middle * ffn_gain).astype(jnp.bfloat16)
    (gate, up), square_sum_mid = rows_to_owner(
        [
            jnp.dot(scaled_mid, w, preferred_element_type=jnp.float32).reshape(seq_count, 2, -1)
            for w in (w_gate, w_up)
        ],
        square_mid,
        jnp.bfloat16,
    )
    scale_mid = lax.rsqrt(square_sum_mid / D + EPSILON)
    hidden = (jax.nn.silu(gate * scale_mid) * (up * scale_mid)).astype(jnp.bfloat16)
    hidden_half = from_everyone(hidden, "seq")
    hidden_rows = from_everyone(hidden_half, "rep").swapaxes(0, 1).reshape(seq_count, -1)
    down_part = from_everyone(
        jnp.dot(hidden_rows, w_down, preferred_element_type=jnp.float32), "head"
    ).sum(axis=0)
    layer = (middle + down_part).astype(jnp.bfloat16)
    layer_out = jnp.dot(
        to_row.T.astype(jnp.bfloat16), layer, preferred_element_type=jnp.float32
    ).astype(jnp.bfloat16)
    return (layer_out, decoded)


def solution(mesh):
    in_specs = (
        P("groups", ("seq", "rep")),
        P(("seq", "rep")),
        P(("seq", "rep")),
        P(("seq", "rep"), "head"),
        P(("seq", "rep"), "head"),
        P(("seq", "rep"), "head"),
        P("head", ("seq", "rep")),
        P(("seq", "rep"), "head"),
        P(("seq", "rep"), "head"),
        P("head", ("seq", "rep")),
        P(None, ("groups", "seq"), "head", "rep", None),
        P("groups"),
        P("groups"),
        P("groups", None),
    )
    out_specs = (P("groups", ("seq", "rep")), P(None, "groups", ("seq", "rep"), "head"))
    return jax.shard_map(shards, mesh=mesh, in_specs=in_specs, out_specs=out_specs, check_vma=False)
```

time: 669 us -> 513 us (0.77)
  waiting for transfers between devices: 323 us -> 175 us
    all_to_all x5 -> x7, blocking collectives: 31.8 us -> 212 us  [the longest x1 115 us: shards(): lax.all_to_all(logical, 'seq', split_axis=0, concat_axis=0, tiled=True)]
    psum x4 -> x0, blocking collectives: 160 us -> none  [by_axis(): value = lax.psum(value, axis)]
    all_to_all x9, waiting for transfers between devices: 323 us -> 175 us  [the longest x1 102 us: shards(): lax.all_to_all(logical, 'seq', split_axis=0, concat_axis=0, tiled=True)]
    all_gather x2 -> x0, blocking collectives: 19.4 us -> none  [the longest x1 9.76 us: sent_together(): filled = lax.all_gather(both, axis, axis=dim, tiled=True)]
    unnamed x42 -> x52, local copies, waits for them, and re-layouts: 18.8 us -> 25.7 us
  transfers between devices with their start and end apart: 9 -> 9, of which waited for: 9 -> 7; matrix products, arithmetic and copies ran while one was open for 7% -> 10% of each run, Pallas kernels for 0% -> 0%
where the time goes in v1:
time: 513 us; the launch traced here: 511 us
  blocking collectives  212 us (41%)
  waiting for transfers between devices  175 us (34%)
  starting transfers between devices  48.1 us (9%)
  local copies, waits for them, and re-layouts  46.6 us (9%)
  other arithmetic  16.4 us (3%)
  matrix products  8.26 us (2%)
  between operations  5.8 us (1%)
    all_to_all x1, blocking collectives, shards(): lax.all_to_all(logical, 'seq', split_axis=0, concat_axis=0, tiled=True)  115 us
    all_to_all x1, waiting for transfers between devices, shards(): lax.all_to_all(logical, 'seq', split_axis=0, concat_axis=0, tiled=True)  102 us
    all_to_all x6, blocking collectives, exchanged(): return lax.all_to_all(tiles, axis, split_axis=0, concat_axis=0, tiled=True)  96.6 us
    all_to_all x6, waiting for transfers between devices, exchanged(): return lax.all_to_all(tiles, axis, split_axis=0, concat_axis=0, tiled=True)  57.4 us
    all_to_all x6, starting transfers between devices, exchanged(): return lax.all_to_all(tiles, axis, split_axis=0, concat_axis=0, tiled=True)  32.1 us
    unnamed x52, local copies, waits for them, and re-layouts  25.7 us
    all_to_all x2, waiting for transfers between devices, shards(): lax.all_to_all(pool_local[side], 'head', split_axis=2, concat_axis=0, til...  15.2 us
  transfers between devices with their start and end apart: 9, of which 7 were waited for; matrix products, arithmetic and copies ran while one was open for 10% of the time, Pallas kernels for 0%

profile of v1, /device:TPU:33, one launch (start us, length us, event | category | flops | bytes accessed | tf_op | source)
XLA Modules:
  0.0 511.4 jit_solution(6550149796238237941)
XLA Ops:
  4.7 45.0 %all_to_all.108 = f32[2,32,896]{2,1,0:T(8,128)S(1)} all-to-all(f32[2,32,896]{2,1,0:T(8,128)S(1)} %maximum_bitcast_fusion.1), channel_id=1, replica_groups=mesh['groups'=2,'seq'=32,'head'=4,'rep'=2] {'rep'}, dimensions={0} | all-to-all | bytes 458752 | tf_op jit(solution)/shard_map/all_to_all | solution.py:21
  50.4 5.5 %all-to-all-start.1 = ((f32[32,1,896]{2,1,0:T(1,128)}), f32[32,1,896]{2,1,0:T(1,128)S(1)}, u32[]{:S(2)}, u32[]{:S(2)}) async-start(f32[32,1,896]{2,1,0:T(1,128)} %broadcast_in_dim.94), calls=%async_computation.1 | async-start | bytes 229376 | tf_op jit(solution)/shard_map/all_to_all | solution.py:21
  61.9 21.7 %all-to-all-done.1 = f32[32,1,896]{2,1,0:T(1,128)S(1)} async-done(((f32[32,1,896]{2,1,0:T(1,128)}), f32[32,1,896]{2,1,0:T(1,128)S(1)}, u32[]{:S(2)}, u32[]{:S(2)}) %all-to-all-start.1) | async-done | bytes 114720 | tf_op jit(solution)/shard_map/all_to_all | solution.py:21
  86.5 7.2 %all-to-all-start.2 = ((bf16[8,4,128]{2,1,0:T(4,128)(2,1)}), bf16[8,4,128]{2,1,0:T(4,128)(2,1)S(1)}, u32[]{:S(2)}, u32[]{:S(2)}) async-start(bf16[8,4,128]{2,1,0:T(4,128)(2,1)} %broadcast_in_dim.95), calls=%async_computation.2 | async-start | bytes 16384 | tf_op jit(solution)/shard_map/all_to_all | solution.py:21
  104.5 9.4 %all_to_all.109 = f32[8,4,384]{2,1,0:T(4,128)S(1)} all-to-all(f32[8,4,384]{2,1,0:T(4,128)S(1)} %pad_maximum_fusion.1), channel_id=1, replica_groups=mesh['groups'=2,'seq'=32,'head'=4,'rep'=2] {'head','rep'}, dimensions={0} | all-to-all | bytes 98304 | tf_op jit(solution)/shard_map/all_to_all | solution.py:21
  117.8 25.0 %all_to_all.110 = bf16[32,2,256]{2,1,0:T(2,128)(2,1)S(1)} all-to-all(bf16[32,2,256]{2,1,0:T(2,128)(2,1)S(1)} %reshape.320), channel_id=1, replica_groups=mesh['groups'=2,'seq'=32,'head'=4,'rep'=2] {'seq'}, dimensions={0} | all-to-all | bytes 65536 | tf_op jit(solution)/shard_map/all_to_all | solution.py:21
  142.8 5.6 %all_to_all.111 = bf16[2,32,512]{2,1,0:T(8,128)(2,1)S(1)} all-to-all(bf16[2,32,512]{2,1,0:T(8,128)(2,1)S(1)} %broadcast_in_dim.102), channel_id=1, replica_groups=mesh['groups'=2,'seq'=32,'head'=4,'rep'=2] {'rep'}, dimensions={0} | all-to-all | bytes 131072 | tf_op jit(solution)/shard_map/all_to_all | solution.py:21
  149.3 3.4 all-to-all-start.6
  155.7 4.4 reshape.330
  162.2 4.9 all_to_all.112
  167.1 4.4 all-to-all-start.14
  178.0 8.0 %all-to-all-done.14 = bf16[4,2,65536]{2,1,0:T(2,128)(2,1)S(1)} async-done(((bf16[4,2,65536]{2,1,0:T(2,128)(2,1)}), bf16[4,2,65536]{2,1,0:T(2,128)(2,1)S(1)}, u32[]{:S(2)}, u32[]{:S(2)}) %all-to-all-start.14) | async-done | bytes 1048608 | tf_op jit(solution)/shard_map/all_to_all | solution.py:121
  186.0 4.8 all-to-all-start.8
  192.2 4.4 reshape.332
  196.6 22.5 %all-to-all-done.8 = bf16[32,2,1024]{2,1,0:T(2,128)(2,1)S(1)} async-done(((bf16[32,2,1024]{2,1,0:T(2,128)(2,1)}), bf16[32,2,1024]{2,1,0:T(2,128)(2,1)S(1)}, u32[]{:S(2)}, u32[]{:S(2)}) %all-to-all-start.8) | async-done | bytes 131104 | tf_op jit(solution)/shard_map/all_to_all | solution.py:21
  219.1 3.6 all-to-all-start.12
  226.8 7.2 %all-to-all-done.12 = bf16[4,2,65536]{2,1,0:T(2,128)(2,1)S(1)} async-done(((bf16[4,2,65536]{2,1,0:T(2,128)(2,1)}), bf16[4,2,65536]{2,1,0:T(2,128)(2,1)S(1)}, u32[]{:S(2)}, u32[]{:S(2)}) %all-to-all-start.12) | async-done | bytes 1048608 | tf_op jit(solution)/shard_map/all_to_all | solution.py:121
  234.0 8.0 %all-to-all-start.9 = ((bf16[32,2,448]{2,1,0:T(2,128)(2,1)}), bf16[32,2,448]{2,1,0:T(2,128)(2,1)S(1)}, u32[]{:S(2)}, u32[]{:S(2)}) async-start(bf16[32,2,448]{2,1,0:T(2,128)(2,1)} %reshape.326), calls=%async_computation.9 | async-start | bytes 131072 | tf_op jit(solution)/shard_map/all_to_all | solution.py:21
  254.8 10.2 %all-to-all-done.9 = bf16[32,2,448]{2,1,0:T(2,128)(2,1)S(1)} async-done(((bf16[32,2,448]{2,1,0:T(2,128)(2,1)}), bf16[32,2,448]{2,1,0:T(2,128)(2,1)S(1)}, u32[]{:S(2)}, u32[]{:S(2)}) %all-to-all-start.9) | async-done | bytes 57376 | tf_op jit(solution)/shard_map/all_to_all | solution.py:21
  265.2 6.7 %all_to_all.113 = bf16[2,32,896]{2,1,0:T(8,128)(2,1)S(1)} all-to-all(bf16[2,32,896]{2,1,0:T(8,128)(2,1)S(1)} %broadcast_in_dim.180), channel_id=1, replica_groups=mesh['groups'=2,'seq'=32,'head'=4,'rep'=2] {'rep'}, dimensions={0} | all-to-all | bytes 229376 | tf_op jit(solution)/shard_map/all_to_all | solution.py:21
  273.8 3.4 all-to-all-start.11
  281.4 115.0 %all_to_all.114 = bf16[32,64,256]{2,1,0:T(8,128)(2,1)S(1)} all-to-all(bf16[32,64,256]{2,1,0:T(8,128)(2,1)S(1)} %get-tuple-element.28), channel_id=1, replica_groups=mesh['groups'=2,'seq'=32,'head'=4,'rep'=2] {'seq'}, dimensions={0} | all-to-all | bytes 2097152 | tf_op jit(solution)/shard_map/all_to_all | solution.py:123
  396.3 8.0 %all-to-all-start.15 = ((bf16[32,64,256]{2,1,0:T(8,128)(2,1)}), bf16[32,64,256]{2,1,0:T(8,128)(2,1)S(1)}, u32[]{:S(2)}, u32[]{:S(2)}) async-start(bf16[32,64,256]{2,1,0:T(8,128)(2,1)} %get-tuple-element.29), calls=%async_computation.15 | async-start | bytes 2097152 | tf_op jit(solution)/shard_map/all_to_all | solution.py:123
  406.7 102.1 %all-to-all-done.15 = bf16[32,64,256]{2,1,0:T(8,128)(2,1)S(1)} async-done(((bf16[32,64,256]{2,1,0:T(8,128)(2,1)}), bf16[32,64,256]{2,1,0:T(8,128)(2,1)S(1)}, u32[]{:S(2)}, u32[]{:S(2)}) %all-to-all-start.15) | async-done | bytes 1048608 | tf_op jit(solution)/shard_map/all_to_all | solution.py:123
  (151 shorter events, 65.4 us)
Async XLA Ops:
  0.6 161.0 %copy-start = (bf16[64,1792]{1,0:T(8,128)(2,1)S(1)}, bf16[64,1792]{1,0:T(8,128)(2,1)}, u32[]{:S(2)}) copy-start(bf16[64,1792]{1,0:T(8,128)(2,1)} %param.24) | copy-start | bytes 688132
  0.6 55.3 %copy-start.9 = (s32[32]{0:T(128)S(1)}, s32[32]{0:T(128)}, u32[]{:S(2)}) copy-start(s32[32]{0:T(128)} %param.28) | copy-start | bytes 388
  0.7 57.9 %copy-start.11 = (s32[32]{0:T(128)S(1)}, s32[32]{0:T(128)}, u32[]{:S(2)}) copy-start(s32[32]{0:T(128)} %param.27) | copy-start | bytes 388
  0.7 60.0 %copy-start.6 = (bf16[2,1,8,64,1024]{4,3,2,1,0:T(8,128)(2,1)S(1)}, bf16[2,1,8,64,1024]{4,3,2,1,0:T(8,128)(2,1)}, u32[]{:S(2)}) copy-start(bf16[2,1,8,64,1024]{4,3,2,1,0:T(8,128)(2,1)} %param.26) | copy-start | bytes 6291460
  50.4 33.2 %all-to-all-start.1 = ((f32[32,1,896]{2,1,0:T(1,128)}), f32[32,1,896]{2,1,0:T(1,128)S(1)}, u32[]{:S(2)}, u32[]{:S(2)}) async-start(f32[32,1,896]{2,1,0:T(1,128)} %broadcast_in_dim.94), calls=%async_computation.1 | async-start | bytes 229376 | tf_op jit(solution)/shard_map/all_to_all | solution.py:21
  60.4 1.5 copy-start.13
  86.5 15.6 %all-to-all-start.2 = ((bf16[8,4,128]{2,1,0:T(4,128)(2,1)}), bf16[8,4,128]{2,1,0:T(4,128)(2,1)S(1)}, u32[]{:S(2)}, u32[]{:S(2)}) async-start(bf16[8,4,128]{2,1,0:T(4,128)(2,1)} %broadcast_in_dim.95), calls=%async_computation.2 | async-start | bytes 16384 | tf_op jit(solution)/shard_map/all_to_all | solution.py:21
  96.1 1.3 copy-start.1
  102.2 46.3 %copy-start.8 = (bf16[1024,64]{0,1:T(8,128)(2,1)S(1)}, bf16[1024,64]{0,1:T(8,128)(2,1)}, u32[]{:S(2)}) copy-start(bf16[1024,64]{0,1:T(8,128)(2,1)} %param.22) | copy-start | bytes 393220
  149.3 10.8 %all-to-all-start.6 = ((f32[4,1,2048]{2,1,0:T(1,128)}), f32[4,1,2048]{2,1,0:T(1,128)S(1)}, u32[]{:S(2)}, u32[]{:S(2)}) async-start(f32[4,1,2048]{2,1,0:T(1,128)} %reshape.322), calls=%async_computation.6 | async-start | bytes 65536 | tf_op jit(solution)/shard_map/all_to_all | solution.py:21
  155.7 5.9 %copy-start.10 = (f32[64]{0:T(128)S(1)}, f32[64]{0:T(128)}, u32[]{:S(2)}) copy-start(f32[64]{0:T(128)} %param.18) | copy-start | bytes 772
  155.7 6.1 %copy-start.7 = (bf16[64,1792]{1,0:T(8,128)(2,1)S(1)}, bf16[64,1792]{1,0:T(8,128)(2,1)}, u32[]{:S(2)}) copy-start(bf16[64,1792]{1,0:T(8,128)(2,1)} %param.23) | copy-start | bytes 688132
  167.1 19.0 %all-to-all-start.14 = ((bf16[4,2,65536]{2,1,0:T(2,128)(2,1)}), bf16[4,2,65536]{2,1,0:T(2,128)(2,1)S(1)}, u32[]{:S(2)}, u32[]{:S(2)}) async-start(bf16[4,2,65536]{2,1,0:T(2,128)(2,1)} %reshape.330), calls=%async_computation.14 | async-start | bytes 2097152 | tf_op jit(solution)/shard_map/all_to_all | solution.py:121
  186.0 33.0 %all-to-all-start.8 = ((bf16[32,2,1024]{2,1,0:T(2,128)(2,1)}), bf16[32,2,1024]{2,1,0:T(2,128)(2,1)S(1)}, u32[]{:S(2)}, u32[]{:S(2)}) async-start(bf16[32,2,1024]{2,1,0:T(2,128)(2,1)} %reshape.324), calls=%async_computation.8 | async-start | bytes 262144 | tf_op jit(solution)/shard_map/all_to_all | solution.py:21
  196.6 45.5 %copy-start.14 = (s32[32]{0:T(128)S(1)}, s32[32]{0:T(128)}, u32[]{:S(2)}) copy-start(s32[32]{0:T(128)} %copy-done.13) | copy-start | bytes 388
  219.1 15.0 %all-to-all-start.12 = ((bf16[4,2,65536]{2,1,0:T(2,128)(2,1)}), bf16[4,2,65536]{2,1,0:T(2,128)(2,1)S(1)}, u32[]{:S(2)}, u32[]{:S(2)}) async-start(bf16[4,2,65536]{2,1,0:T(2,128)(2,1)} %reshape.332), calls=%async_computation.12 | async-start | bytes 2097152 | tf_op jit(solution)/shard_map/all_to_all | solution.py:121
  234.0 8.0 %copy-start.2 = (bf16[4,2,65536]{2,1,0:T(2,128)(2,1)}, bf16[4,2,65536]{2,1,0:T(2,128)(2,1)S(1)}, u32[]{:S(2)}) copy-start(bf16[4,2,65536]{2,1,0:T(2,128)(2,1)S(1)} %all-to-all-done.12) | copy-start | bytes 3145732
  234.0 31.0 %all-to-all-start.9 = ((bf16[32,2,448]{2,1,0:T(2,128)(2,1)}), bf16[32,2,448]{2,1,0:T(2,128)(2,1)S(1)}, u32[]{:S(2)}, u32[]{:S(2)}) async-start(bf16[32,2,448]{2,1,0:T(2,128)(2,1)} %reshape.326), calls=%async_computation.9 | async-start | bytes 131072 | tf_op jit(solution)/shard_map/all_to_all | solution.py:21
  243.5 4.9 copy-start.3
  251.7 1.5 copy-start.4
  252.9 1.3 copy-start.5
  273.8 7.6 %all-to-all-start.11 = ((f32[4,1,2048]{2,1,0:T(1,128)}), f32[4,1,2048]{2,1,0:T(1,128)S(1)}, u32[]{:S(2)}, u32[]{:S(2)}) async-start(f32[4,1,2048]{2,1,0:T(1,128)} %reshape.328), calls=%async_computation.11 | async-start | bytes 65536 | tf_op jit(solution)/shard_map/all_to_all | solution.py:21
  281.3 123.0 %copy-start.12 = (s32[32]{0:T(128)S(1)}, s32[32]{0:T(128)}, u32[]{:S(2)}) copy-start(s32[32]{0:T(128)} %param.27) | copy-start | bytes 388
  396.3 112.5 %all-to-all-start.15 = ((bf16[32,64,256]{2,1,0:T(8,128)(2,1)}), bf16[32,64,256]{2,1,0:T(8,128)(2,1)S(1)}, u32[]{:S(2)}, u32[]{:S(2)}) async-start(bf16[32,64,256]{2,1,0:T(8,128)(2,1)} %get-tuple-element.29), calls=%async_computation.15 | async-start | bytes 2097152 | tf_op jit(solution)/shard_map/all_to_all | solution.py:123

commit v2 on v1

v2 whole, which is shorter than its diff:
```python
import functools
import math

import jax
import jax.numpy as jnp
from jax import lax
from jax.experimental import pallas as pl
from jax.experimental.pallas import tpu as pltpu
from jax.sharding import PartitionSpec as P

D = 4096
H = 32
KVH = 8
HD = 128
BLK = 128

EPSILON = 1e-05
ROPE_LOG = math.log(500000.0)
FLOOR_SCORE = -1e30
MESH = pl.DeviceIdType.MESH
BF16 = jnp.bfloat16
F32 = jnp.float32


def send(src, dst, send_sem, recv_sem, **where):
    pltpu.make_async_remote_copy(
        src_ref=src,
        dst_ref=dst,
        send_sem=send_sem,
        recv_sem=recv_sem,
        device_id=where,
        device_id_type=MESH,
    ).start()


def drain(ref, sem):
    pltpu.make_async_copy(ref, ref, sem).wait()


def dot(a, b):
    return jnp.dot(a, b, preferred_element_type=F32)


def both_parts(value):
    lead = value.astype(BF16)
    rest = (value - lead.astype(F32)).astype(BF16)
    return jnp.concatenate([lead, rest], axis=0)


def folded(product):
    rows = product.shape[0] // 2
    return product[:rows] + product[rows:]


def kernel(
    n_seq, n_head, n_rep,
    tok, again, fgain, wq, wk, wv, wo, wg, wu, wd, kv, use, turn, table, prow, lens,
    layer_out, decoded,
    xk, xv, zk, zv, rk, rv,
    own1, far1, got1, row1, tile3, state4, got4, swap5, got5, ag5, wide,
    part6, own7, far7, got7, out8, row8, ag9, pair9, part11,
    s_send, s_recv,
):
    z = lax.axis_index("seq")
    h = lax.axis_index("head")
    r = lax.axis_index("rep")
    other = 1 - r
    j = h * n_rep + r
    n_kv = n_head * n_rep
    rows = n_seq
    slots = kv.shape[1]
    half = kv.shape[2]
    width = xk.shape[2]

    barrier = pltpu.get_barrier_semaphore()

    def greet_seq(d, _):
        pl.semaphore_signal(
            barrier, inc=1, device_id={"seq": lax.rem(z + d, n_seq)}, device_id_type=MESH
        )
        return 0

    lax.fori_loop(1, n_seq, greet_seq, 0)
    for t in range(1, n_kv):
        peer = lax.rem(j + t, n_kv)
        pl.semaphore_signal(
            barrier,
            inc=1,
            device_id={"head": peer // n_rep, "rep": peer % n_rep},
            device_id_type=MESH,
        )

    x = tok[...]
    square = jnp.broadcast_to(jnp.sum(x * x, axis=1, keepdims=True), (rows, HD))
    y = both_parts(x * again[...])
    pq, pk, pv = (folded(dot(y, w[...])) for w in (wq, wk, wv))
    qn = pq.shape[1] // n_rep // HD
    for side, buf in ((0, own1), (1, far1)):
        mine = (r == 0) if side == 0 else (r != 0)
        for c in range(qn):
            buf[:, c, :] = jnp.where(
                mine, pq[:, c * HD : (c + 1) * HD], pq[:, (qn + c) * HD : (qn + c + 1) * HD]
            )
        buf[:, qn, :] = jnp.where(mine, pk[:, :HD], pk[:, HD:])
        buf[:, qn + 1, :] = jnp.where(mine, pv[:, :HD], pv[:, HD:])
        buf[:, qn + 2, :] = square
        buf[:, qn + 3, :] = jnp.zeros((rows, HD), F32)

    pl.semaphore_wait(barrier, n_seq - 1 + n_kv - 1)

    send(far1, got1, s_send.at[0], s_recv.at[0], rep=other)

    for c, box in ((0, xk), (1, xv)):
        for t in range(1, n_head):
            peer = lax.rem(h + t, n_head)
            send(
                kv.at[c, :, :, pl.ds(pl.multiple_of(peer * width, width), width)],
                box.at[pl.ds(h * slots, slots)],
                s_send.at[1 + c],
                s_recv.at[1 + c],
                head=peer,
            )
        box[pl.ds(h * slots, slots)] = kv[
            c, :, :, pl.ds(pl.multiple_of(h * width, width), width)
        ]

    drain(got1, s_recv.at[0])
    own1[...] = own1[...] + got1[...]

    def send_seq(src_of, dst, which, lo, hi):
        def body(d, _):
            peer = lax.rem(z + d, n_seq)
            send(src_of(peer), dst.at[z], s_send.at[which], s_recv.at[which], seq=peer)
            back = lax.rem(z + n_seq - d, n_seq)

            @pl.when(d * 2 != n_seq)
            def _():
                send(src_of(back), dst.at[z], s_send.at[which], s_recv.at[which], seq=back)

            return 0

        lax.fori_loop(lo, hi, body, 0)

    reach = n_seq // 2 + 1

    def all_rows(ref):
        return ref.at[pl.ds(0, n_seq - 1)]

    send_seq(lambda p: own1.at[p], row1, 3, 1, reach)
    row1[z] = own1[z]

    drain(all_rows(row1), s_recv.at[3])
    total = jnp.sum(row1[...], axis=0)
    scale = lax.rsqrt(total[qn + 2 : qn + 3, 0:1] / D + EPSILON)
    total = total * scale
    line = lax.broadcasted_iota(jnp.int32, (8, HD), 0)
    turned = total * turn[0:1, :] + pltpu.roll(total, HD // 2, 1) * turn[1:2, :]
    mine = jnp.where(line <= qn, turned, jnp.where(line == qn + 1, total, 0.0))
    mine = mine.astype(BF16).astype(F32)
    tile3[j] = mine
    for t in range(1, n_kv):
        peer = lax.rem(j + t, n_kv)
        send(
            tile3.at[j], tile3.at[j], s_send.at[4], s_recv.at[4],
            head=peer // n_rep, rep=peer % n_rep,
        )
    drain(tile3.at[pl.ds(0, n_kv - 1)], s_recv.at[4])

    factor = 1.0 / math.sqrt(HD)
    live = use[...] > 0.5
    lane = lax.broadcasted_iota(jnp.int32, (8, HD), 1)
    for g in range(n_kv):
        keys = kv[0, :, :, g * HD : (g + 1) * HD].reshape(slots * half, HD)
        values = kv[1, :, :, g * HD : (g + 1) * HD].reshape(slots * half, HD)
        scores = (
            lax.dot_general(
                tile3[g].astype(BF16), keys, (((1,), (1,)), ((), ())), preferred_element_type=F32
            )
            * factor
        )
        scores = jnp.where(live, scores, FLOOR_SCORE)
        top = jnp.max(scores, axis=1, keepdims=True)
        weights = jnp.where(live, jnp.exp(scores - top), 0.0)
        mass = jnp.sum(weights, axis=1, keepdims=True)
        state4[g, 0:8, :] = dot(weights.astype(BF16), values)
        state4[g, 8:16, :] = jnp.where(lane < HD // 2, top, mass)
    for t in range(1, n_kv):
        peer = lax.rem(j + t, n_kv)
        send(
            state4.at[peer], got4.at[j], s_send.at[5], s_recv.at[5],
            head=peer // n_rep, rep=peer % n_rep,
        )
    got4[j] = state4[j]
    drain(got4.at[pl.ds(0, n_kv - 1)], s_recv.at[5])
    own_score = jnp.sum(mine * mine[qn : qn + 1, :], axis=1, keepdims=True) * factor
    top = own_score
    for s in range(n_kv):
        top = jnp.maximum(top, got4[s, 8:16, 0:1])
    own = jnp.exp(own_score - top)
    mass = own
    mixed = own * mine[qn + 1 : qn + 2, :]
    for s in range(n_kv):
        kept = jnp.exp(got4[s, 8:16, 0:1] - top)
        mass = mass + kept * got4[s, 8:16, HD // 2 : HD // 2 + 1]
        mixed = mixed + kept * got4[s, 0:8, :]
    swap5[...] = mixed / mass
    send(swap5, got5, s_send.at[6], s_recv.at[6], rep=other)

    drain(xk.at[pl.ds(0, (n_head - 1) * slots)], s_recv.at[1])

    def order_keys(b, _):
        zk[b] = xk[table[b]]
        return 0

    lax.fori_loop(0, n_seq, order_keys, 0)

    drain(got5, s_recv.at[6])
    first = jnp.where(r == 0, swap5[...], got5[...])
    second = jnp.where(r == 0, got5[...], swap5[...])
    ag5[z] = jnp.where(line < qn, first, pltpu.roll(second, qn, 0)).astype(BF16)
    send_seq(lambda p: ag5.at[z], ag5, 7, 1, reach)
    send_seq(lambda p: zk.at[p], rk, 8, 1, reach)
    rk[z] = zk[z]

    drain(xv.at[pl.ds(0, (n_head - 1) * slots)], s_recv.at[2])

    def order_values(b, _):
        zv[b] = xv[table[b]]
        return 0

    lax.fori_loop(0, n_seq, order_values, 0)

    drain(all_rows(ag5), s_recv.at[7])
    wide[...] = ag5[...].astype(F32)
    acc = dot(wide[:, 0, :].astype(BF16), wo[0:HD, :])
    for g in range(1, n_rep * qn):
        acc = acc + dot(wide[:, g, :].astype(BF16), wo[g * HD : (g + 1) * HD, :])
    pad = jnp.zeros((rows, HD - acc.shape[1]), F32)
    part6[h] = jnp.concatenate([acc, pad], axis=1)
    for t in range(1, n_head):
        peer = lax.rem(h + t, n_head)
        send(part6.at[h], part6.at[h], s_send.at[9], s_recv.at[9], head=peer)
    drain(part6.at[pl.ds(0, n_head - 1)], s_recv.at[9])
    proj = part6[0]
    for s in range(1, n_head):
        proj = proj + part6[s]
    middle = x + proj[:, : x.shape[1]]

    square = jnp.broadcast_to(jnp.sum(middle * middle, axis=1, keepdims=True), (rows, HD))
    y = both_parts(middle * fgain[...])
    fn = wg.shape[1] // n_rep // HD
    for w, at in ((wg, 0), (wu, 8)):
        p = folded(dot(y, w[...]))
        for side, buf in ((0, own7), (1, far7)):
            here = (r == 0) if side == 0 else (r != 0)
            for c in range(fn):
                buf[:, at + c, :] = jnp.where(
                    here, p[:, c * HD : (c + 1) * HD], p[:, (fn + c) * HD : (fn + c + 1) * HD]
                )
            for c in range(fn, 8):
                buf[:, at + c, :] = square
    send(far7, got7, s_send.at[10], s_recv.at[10], rep=other)
    drain(got7, s_recv.at[10])
    own7[...] = own7[...] + got7[...]
    square = own7[:, 7, :]
    own7[:, 15, :] = square - square.astype(BF16).astype(F32)
    out8[...] = own7[...].astype(BF16)
    send_seq(lambda p: out8.at[p], row8, 11, 1, reach)
    row8[z] = out8[z]

    cut = reach - n_seq // 8
    send_seq(lambda p: zv.at[p], rv, 12, cut, reach)

    drain(all_rows(row8), s_recv.at[11])
    total = jnp.sum(row8[...].astype(F32), axis=0)
    scale = lax.rsqrt((total[7:8, 0:1] + total[15:16, 0:1]) / D + EPSILON)
    gate = total[0:8] * scale
    up = total[8:16] * scale
    hidden = gate / (1.0 + jnp.exp(-gate)) * up
    ag9[z] = jnp.where(line < fn, hidden, 0.0).astype(BF16)
    send_seq(lambda p: ag9.at[z], ag9, 13, 1, reach)
    send_seq(lambda p: zv.at[p], rv, 12, 1, cut)
    rv[z] = zv[z]

    drain(all_rows(ag9), s_recv.at[13])
    send(ag9, pair9, s_send.at[14], s_recv.at[14], rep=other)

    def down(ref, which):
        wide[...] = ref[...].astype(F32)
        acc = jnp.zeros((rows, x.shape[1]), F32)
        for c in range(fn):
            at = pl.multiple_of((which * fn + c) * HD, HD)
            acc = acc + dot(wide[:, c, :].astype(BF16), wd[pl.ds(at, HD), :])
        return acc

    acc = down(ag9, r)
    drain(pair9, s_recv.at[14])
    acc = acc + down(pair9, other)
    part11[h] = jnp.concatenate([acc, pad], axis=1)
    for t in range(1, n_head):
        peer = lax.rem(h + t, n_head)
        send(part11.at[h], part11.at[h], s_send.at[15], s_recv.at[15], head=peer)
    drain(part11.at[pl.ds(0, n_head - 1)], s_recv.at[15])
    proj = part11[0]
    for s in range(1, n_head):
        proj = proj + part11[s]
    layer_out[...] = middle + proj[:, : x.shape[1]]

    here = z * BLK + r * half + lax.broadcasted_iota(jnp.int32, (half, width), 0)
    for c, box, sem in ((0, rk, 8), (1, rv, 12)):
        drain(all_rows(box), s_recv.at[sem])

        def place(i, _):
            found = box[prow[i]]
            decoded[c, i] = jnp.where(here < lens[i], found, jnp.zeros((), found.dtype))
            return 0

        lax.fori_loop(0, rows, place, 0)

    drain(far1, s_send.at[0])
    for c, box in ((0, xk), (1, xv)):
        drain(box.at[pl.ds(0, (n_head - 1) * slots)], s_send.at[1 + c])
    drain(all_rows(own1), s_send.at[3])
    drain(tile3.at[pl.ds(0, n_kv - 1)], s_send.at[4])
    drain(state4.at[pl.ds(0, n_kv - 1)], s_send.at[5])
    drain(swap5, s_send.at[6])
    drain(all_rows(ag5), s_send.at[7])
    drain(all_rows(zk), s_send.at[8])
    drain(part6.at[pl.ds(0, n_head - 1)], s_send.at[9])
    drain(far7, s_send.at[10])
    drain(all_rows(out8), s_send.at[11])
    drain(all_rows(zv), s_send.at[12])
    drain(all_rows(ag9), s_send.at[13])
    drain(ag9, s_send.at[14])
    drain(part11.at[pl.ds(0, n_head - 1)], s_send.at[15])


def shards(
    tokens,
    attn_gain,
    ffn_gain,
    w_query,
    w_key,
    w_value,
    w_out,
    w_gate,
    w_up,
    w_down,
    kv_pool,
    lengths,
    pool_row,
    block_table,
):
    rows, features = tokens.shape
    n_seq, n_head, n_rep = (lax.axis_size(a) for a in ("seq", "head", "rep"))
    slots, half = kv_pool.shape[2:4]
    width = kv_pool.shape[4] // n_head
    row_here = lax.axis_index("seq")
    head_here = lax.axis_index("head")
    rep_here = lax.axis_index("rep")
    seq_ids = jnp.arange(rows, dtype=jnp.int32)
    to_row = pool_row[None, :] == seq_ids[:, None]
    owner = pool_row == row_here
    table_row = jnp.sum(jnp.where(owner[:, None], block_table, 0), axis=0)
    length_here = jnp.sum(jnp.where(owner, lengths, 0))

    residual = jnp.dot(to_row.astype(BF16), tokens, preferred_element_type=F32)
    block_ids = jnp.arange(table_row.shape[0], dtype=jnp.int32)
    slot_ids = head_here * slots + jnp.arange(slots, dtype=jnp.int32)
    block_of_slot = jnp.sum(
        jnp.where(table_row[None, :] == slot_ids[:, None], block_ids[None, :], 0), axis=1
    )
    token_pos = (
        block_of_slot[:, None] * BLK
        + rep_here * half
        + jnp.arange(half, dtype=jnp.int32)[None, :]
    )
    usable = (token_pos < length_here).astype(F32).reshape(1, slots * half)
    freq_table = jnp.exp(jnp.arange(HD // 2, dtype=F32) * (-2.0 * ROPE_LOG / HD))
    angles = length_here.astype(F32) * freq_table
    sine = jnp.sin(angles)
    cosine = jnp.cos(angles)
    turn = jnp.stack(
        [jnp.concatenate([cosine, cosine]), jnp.concatenate([-sine, sine])]
    )

    vmem = pl.BlockSpec(memory_space=pltpu.VMEM)
    smem = pl.BlockSpec(memory_space=pltpu.SMEM)
    ring = (n_seq, half, width)
    n_kv = n_head * n_rep
    layer, decoded = pl.pallas_call(
        functools.partial(kernel, n_seq, n_head, n_rep),
        out_shape=(
            jax.ShapeDtypeStruct((rows, features), F32),
            jax.ShapeDtypeStruct((2, rows, half, width), BF16),
        ),
        in_specs=[vmem] * 13 + [smem] * 3,
        out_specs=(vmem, vmem),
        scratch_shapes=[
            pltpu.VMEM((n_head * slots, half, width), BF16),
            pltpu.VMEM((n_head * slots, half, width), BF16),
            pltpu.VMEM(ring, BF16),
            pltpu.VMEM(ring, BF16),
            pltpu.VMEM(ring, BF16),
            pltpu.VMEM(ring, BF16),
            pltpu.VMEM((rows, 8, HD), F32),
            pltpu.VMEM((rows, 8, HD), F32),
            pltpu.VMEM((rows, 8, HD), F32),
            pltpu.VMEM((rows, 8, HD), F32),
            pltpu.VMEM((n_kv, 8, HD), F32),
            pltpu.VMEM((n_kv, 16, HD), F32),
            pltpu.VMEM((n_kv, 16, HD), F32),
            pltpu.VMEM((8, HD), F32),
            pltpu.VMEM((8, HD), F32),
            pltpu.VMEM((rows, 8, HD), BF16),
            pltpu.VMEM((rows, 8, HD), F32),
            pltpu.VMEM((n_head, rows, HD), F32),
            pltpu.VMEM((rows, 16, HD), F32),
            pltpu.VMEM((rows, 16, HD), F32),
            pltpu.VMEM((rows, 16, HD), F32),
            pltpu.VMEM((rows, 16, HD), BF16),
            pltpu.VMEM((rows, 16, HD), BF16),
            pltpu.VMEM((rows, 8, HD), BF16),
            pltpu.VMEM((rows, 8, HD), BF16),
            pltpu.VMEM((n_head, rows, HD), F32),
            pltpu.SemaphoreType.DMA((16,)),
            pltpu.SemaphoreType.DMA((16,)),
        ],
        compiler_params=pltpu.CompilerParams(
            collective_id=0, has_side_effects=True, vmem_limit_bytes=48 * 1024 * 1024
        ),
        name="decode_layer",
    )(
        residual,
        attn_gain[None, :],
        ffn_gain[None, :],
        w_query,
        w_key,
        w_value,
        w_out,
        w_gate,
        w_up,
        w_down,
        kv_pool[:, 0],
        usable,
        turn,
        table_row,
        pool_row,
        lengths,
    )
    layer_out = jnp.dot(
        to_row.T.astype(BF16), layer.astype(BF16), preferred_element_type=F32
    ).astype(BF16)
    return (layer_out, decoded)


def solution(mesh):
    in_specs = (
        P("groups", ("seq", "rep")),
        P(("seq", "rep")),
        P(("seq", "rep")),
        P(("seq", "rep"), "head"),
        P(("seq", "rep"), "head"),
        P(("seq", "rep"), "head"),
        P("head", ("seq", "rep")),
        P(("seq", "rep"), "head"),
        P(("seq", "rep"), "head"),
        P("head", ("seq", "rep")),
        P(None, ("groups", "seq"), "head", "rep", None),
        P("groups"),
        P("groups"),
        P("groups", None),
    )
    out_specs = (P("groups", ("seq", "rep")), P(None, "groups", ("seq", "rep"), "head"))
    return jax.shard_map(shards, mesh=mesh, in_specs=in_specs, out_specs=out_specs, check_vma=False)
```

time: 513 us -> 312 us (0.61)
  the two profiles are of different devices: /device:TPU:33 before, /device:TPU:168 now
where the time goes in v2:
time: 312 us; the launch traced here: 311 us
  Pallas kernels  293 us (94%)
  local copies, waits for them, and re-layouts  12.2 us (4%)
  other arithmetic  3.31 us (1%)
    pallas_call x1, Pallas kernels, shards(): pl.pallas_call(functools.partial(kernel, n_seq, n_head, n_rep), out_shape...  293 us
    unnamed x25, local copies, waits for them, and re-layouts  12.1 us

profile of v2, /device:TPU:168, one launch (start us, length us, event | category | flops | bytes accessed | tf_op | source)
XLA Modules:
  0.0 311.4 jit_solution(4957058293789510812)
XLA Ops:
  0.7 1.3 select_reduce_fusion.2
  2.6 0.8 select_reduce_fusion.table
  3.4 0.2 select_reduce_fusion.1
  3.6 0.1 fusion.7
  3.7 0.1 maximum_bitcast_fusion.1
  3.8 0.1 maximum_bitcast_fusion
  3.9 0.7 fusion.4
  4.6 0.1 reshape.50.use
  4.7 0.8 fusion.tok
  5.5 1.1 copy.18.wo
  6.6 1.2 copy.19.wd
  7.8 1.6 copy-done.1
  9.4 0.9 copy-done.2
  10.3 0.9 copy-done.3
  11.3 0.9 copy-done.4
  12.2 0.8 copy-done.5
  12.9 0.8 copy-done.6
  13.7 0.7 copy-done.7
  14.3 0.7 copy-done.8
  15.0 0.7 copy-done.9
  15.6 0.7 copy-done.10
  16.3 293.0 %decode_layer.1 = (f32[32,64]{1,0:T(8,128)S(1)}, bf16[2,32,64,256]{3,2,1,0:T(8,128)(2,1)S(1)}) custom-call(f32[32,64]{1,0:T(8,128)S(1)} %fusion.tok, f32[1,64]{1,0:T(1,128)S(1)} %bitcast.9, f32[1,64]{1,0:T(1,128)S(1)} %bitcast.10, bf16[64,1024]{1,0:T(8,128)(2,1)S(1)} %copy-done.4, bf16[64,256]{1,0:T(8,128)(2,1)S(1)} %copy-done.5, ...), custom_call_target="tpu_custom_call" | custom-call | tf_op jit(solution)/shard_map/decode_layer/pallas_call | solution.py:391
  309.3 0.8 convolution_convert_fusion
  310.1 1.3 copy.21
  (16 shorter events, 0.1 us)
Async XLA Ops:
  0.6 4.1 %copy-start = (bf16[32,64]{1,0:T(8,128)(2,1)S(1)}, bf16[32,64]{1,0:T(8,128)(2,1)}, u32[]{:S(2)}) copy-start(bf16[32,64]{1,0:T(8,128)(2,1)} %param.14) | copy-start | bytes 12292
  7.8 1.6 copy-start.1
  9.4 0.9 copy-start.2
  10.3 0.9 copy-start.3
  11.3 0.9 copy-start.4
  12.2 0.8 copy-start.5
  12.9 0.8 copy-start.6
  13.7 0.7 copy-start.7
  14.3 0.7 copy-start.8
  15.0 0.7 copy-start.9
  15.6 0.7 copy-start.10

commit v3 on v2

v3 whole, which is shorter than its diff:
```python
import functools
import math

import jax
import jax.numpy as jnp
from jax import lax
from jax.experimental import pallas as pl
from jax.experimental.pallas import tpu as pltpu
from jax.sharding import PartitionSpec as P

D = 4096
H = 32
KVH = 8
HD = 128
BLK = 128

EPSILON = 1e-05
ROPE_LOG = math.log(500000.0)
FLOOR_SCORE = -1e30
MESH = pl.DeviceIdType.MESH
BF16 = jnp.bfloat16
F32 = jnp.float32


def send(src, dst, send_sem, recv_sem, **where):
    pltpu.make_async_remote_copy(
        src_ref=src,
        dst_ref=dst,
        send_sem=send_sem,
        recv_sem=recv_sem,
        device_id=where,
        device_id_type=MESH,
    ).start()


def drain(ref, sem):
    pltpu.make_async_copy(ref, ref, sem).wait()


def dot(a, b):
    return jnp.dot(a, b, preferred_element_type=F32)


def across(a, b):
    return lax.dot_general(a, b, (((1,), (1,)), ((), ())), preferred_element_type=F32)


def both_parts(value):
    lead = value.astype(BF16)
    rest = (value - lead.astype(F32)).astype(BF16)
    return jnp.concatenate([lead, rest], axis=0)


def folded(product):
    rows = product.shape[0] // 2
    return product[:rows] + product[rows:]


def kernel(n_seq, n_head, n_rep, near, pieces, *refs):
    (
        tok_h, pvec_h, again_h, fgain_h, turn_h, wq_h, wk_h, wv_h, kv_h, wo_h, wg_h, wu_h, wd_h,
        table, prow, lens,
        layer_out, decoded,
        tok, pvec, again, fgain, turn, wq, wk, wv, kv, wo, wg, wu, wd,
    ) = refs[:31]
    count = 2 * pieces
    pool, ordered, arrived = (refs[31 + k * count : 31 + (k + 1) * count] for k in range(3))
    (
        own1, far1, got1, near1, part1, row1, tile3, state4, got4, swap5, got5, ag5, wide,
        part6, own7, far7, got7, near8, part8, row8, ag9, pair9, part11,
        s_send, s_recv, s_load, b_xsend, b_xrecv, b_send, b_recv,
    ) = refs[31 + 3 * count :]
    z = lax.axis_index("seq")
    h = lax.axis_index("head")
    r = lax.axis_index("rep")
    other = 1 - r
    j = h * n_rep + r
    n_kv = n_head * n_rep
    rows = n_seq
    blocks = n_seq // near
    k_here, g_here = z % near, z // near
    slots = kv.shape[1]
    half = kv.shape[2]
    held = slots * half
    some = half // pieces
    width = decoded.shape[3]

    loads = [
        pltpu.make_async_copy(src, dst, s_load.at[k])
        for k, (src, dst) in enumerate(
            zip(
                (kv_h.at[:, 0], tok_h, pvec_h, again_h, fgain_h, turn_h, wq_h, wk_h, wv_h,
                 wo_h, wg_h, wu_h, wd_h),
                (kv, tok, pvec, again, fgain, turn, wq, wk, wv, wo, wg, wu, wd),
            )
        )
    ]
    for load in loads:
        load.start()

    barrier = pltpu.get_barrier_semaphore()

    def greet_seq(d, _):
        pl.semaphore_signal(
            barrier, inc=1, device_id={"seq": lax.rem(z + d, n_seq)}, device_id_type=MESH
        )
        return 0

    lax.fori_loop(1, n_seq, greet_seq, 0)
    for t in range(1, n_kv):
        peer = lax.rem(j + t, n_kv)
        pl.semaphore_signal(
            barrier,
            inc=1,
            device_id={"head": peer // n_rep, "rep": peer % n_rep},
            device_id_type=MESH,
        )
    loads[0].wait()
    pl.semaphore_wait(barrier, n_seq - 1 + n_kv - 1)

    def columns(q, owner):
        return (
            q // pieces,
            slice(None),
            pl.ds((q % pieces) * some, some),
            pl.ds(pl.multiple_of(owner * width, width), width),
        )

    for q in range(count):
        for t in range(1, n_head):
            peer = lax.rem(h + t, n_head)
            send(
                kv.at[columns(q, peer)],
                pool[q].at[pl.ds(h * slots, slots)],
                b_xsend.at[q],
                b_xrecv.at[q],
                head=peer,
            )

    for load in loads[1:9]:
        load.wait()
    at = lax.broadcasted_iota(jnp.int32, (rows, rows), 0)
    to_row = (at % blocks) * near + at // blocks == pvec[...]
    to_row = to_row.astype(F32).astype(BF16)
    x = dot(to_row, tok[...])
    square = jnp.broadcast_to(jnp.sum(x * x, axis=1, keepdims=True), (rows, HD))
    y = both_parts(x * again[...])
    pq, pk, pv = (folded(dot(y, w[...])) for w in (wq, wk, wv))
    qn = pq.shape[1] // n_rep // HD
    for side, buf in ((1, far1), (0, own1)):
        mine = (r == 0) if side == 0 else (r != 0)
        for c in range(qn):
            buf[:, c, :] = jnp.where(
                mine, pq[:, c * HD : (c + 1) * HD], pq[:, (qn + c) * HD : (qn + c + 1) * HD]
            )
        buf[:, qn, :] = jnp.where(mine, pk[:, :HD], pk[:, HD:])
        buf[:, qn + 1, :] = jnp.where(mine, pv[:, :HD], pv[:, HD:])
        buf[:, qn + 2, :] = square
        buf[:, qn + 3, :] = jnp.zeros((rows, HD), F32)
        if side == 1:
            send(far1, got1, s_send.at[0], s_recv.at[0], rep=other)

    def mates(part_of, dst, which):
        for t in range(1, near):
            peer = lax.rem(k_here + t, near)
            send(
                part_of(peer), dst, s_send.at[which], s_recv.at[which], seq=g_here * near + peer
            )

    def across_runs(part_of, dst, which):
        for t in range(1, blocks):
            peer = lax.rem(g_here + t, blocks)
            send(
                part_of(peer), dst, s_send.at[which], s_recv.at[which], seq=peer * near + k_here
            )

    def of_class(ref, k):
        return ref.at[pl.ds(k * blocks, blocks)]

    drain(got1, s_recv.at[0])
    own1[...] = own1[...] + got1[...]
    mates(lambda k: of_class(own1, k), near1.at[k_here], 1)
    near1[k_here] = own1[pl.ds(k_here * blocks, blocks)]
    drain(near1.at[pl.ds(0, near - 1)], s_recv.at[1])
    part1[...] = jnp.sum(near1[...], axis=0)
    across_runs(lambda g: part1.at[g], row1.at[g_here], 2)
    row1[g_here] = part1[g_here]

    owner = lax.fori_loop(0, rows, lambda i, at: jnp.where(prow[i] == z, i, at), 0)
    length = lens[owner]

    def put_in_order(q):
        pool[q][pl.ds(h * slots, slots)] = kv[columns(q, h)]
        drain(pool[q].at[pl.ds(0, (n_head - 1) * slots)], b_xrecv.at[q])

        def one(b, _):
            ordered[q][b] = pool[q][table[owner, b]]
            return 0

        lax.fori_loop(0, n_seq, one, 0)
        arrived[q][z] = ordered[q][z]

    reach = n_seq // 2 + 1

    def bulk(q, lo, hi):
        def body(d, _):
            peer = lax.rem(z + d, n_seq)
            send(ordered[q].at[peer], arrived[q].at[z], b_send.at[q], b_recv.at[q], seq=peer)
            back = lax.rem(z + n_seq - d, n_seq)

            @pl.when(d * 2 != n_seq)
            def _():
                send(ordered[q].at[back], arrived[q].at[z], b_send.at[q], b_recv.at[q], seq=back)

            return 0

        lax.fori_loop(lo, hi, body, 0)

    cuts = (1, 1 + n_seq * 9 // 32, 1 + n_seq * 13 // 32, reach)

    put_in_order(0)
    bulk(0, 1, reach)

    slot_of = lax.broadcasted_iota(jnp.int32, (1, held), 1) // half
    place_of = lax.broadcasted_iota(jnp.int32, (1, held), 1) % half

    def note_block(b, at):
        return jnp.where(slot_of + h * slots == table[owner, b], b, at)

    block_of = lax.fori_loop(0, n_seq, note_block, jnp.zeros((1, held), jnp.int32))
    live = block_of * BLK + r * half + place_of < length

    drain(row1.at[pl.ds(0, blocks - 1)], s_recv.at[2])
    total = jnp.sum(row1[...], axis=0)
    scale = lax.rsqrt(total[qn + 2 : qn + 3, 0:1] / D + EPSILON)
    total = total * scale
    line = lax.broadcasted_iota(jnp.int32, (8, HD), 0)
    turned = total * turn[0:1, :] + pltpu.roll(total, HD // 2, 1) * turn[1:2, :]
    mine = jnp.where(line <= qn, turned, jnp.where(line == qn + 1, total, 0.0))
    mine = mine.astype(BF16).astype(F32)
    tile3[j] = mine
    for t in range(1, n_kv):
        peer = lax.rem(j + t, n_kv)
        send(
            tile3.at[j], tile3.at[j], s_send.at[3], s_recv.at[3],
            head=peer // n_rep, rep=peer % n_rep,
        )
    drain(tile3.at[pl.ds(0, n_kv - 1)], s_recv.at[3])

    factor = 1.0 / math.sqrt(HD)
    lane = lax.broadcasted_iota(jnp.int32, (8, HD), 1)
    for g in range(n_kv):
        keys = kv[0, :, :, g * HD : (g + 1) * HD].reshape(held, HD)
        values = kv[1, :, :, g * HD : (g + 1) * HD].reshape(held, HD)
        scores = across(tile3[g].astype(BF16), keys) * factor
        scores = jnp.where(live, scores, FLOOR_SCORE)
        top = jnp.max(scores, axis=1, keepdims=True)
        weights = jnp.where(live, jnp.exp(scores - top), 0.0)
        mass = jnp.sum(weights, axis=1, keepdims=True)
        state4[g, 0:8, :] = dot(weights.astype(BF16), values)
        state4[g, 8:16, :] = jnp.where(lane < HD // 2, top, mass)
    for t in range(1, n_kv):
        peer = lax.rem(j + t, n_kv)
        send(
            state4.at[peer], got4.at[j], s_send.at[4], s_recv.at[4],
            head=peer // n_rep, rep=peer % n_rep,
        )
    got4[j] = state4[j]
    put_in_order(1)
    drain(got4.at[pl.ds(0, n_kv - 1)], s_recv.at[4])
    own_score = jnp.sum(mine * mine[qn : qn + 1, :], axis=1, keepdims=True) * factor
    top = own_score
    for s in range(n_kv):
        top = jnp.maximum(top, got4[s, 8:16, 0:1])
    own = jnp.exp(own_score - top)
    mass = own
    mixed = own * mine[qn + 1 : qn + 2, :]
    for s in range(n_kv):
        kept = jnp.exp(got4[s, 8:16, 0:1] - top)
        mass = mass + kept * got4[s, 8:16, HD // 2 : HD // 2 + 1]
        mixed = mixed + kept * got4[s, 0:8, :]
    swap5[...] = mixed / mass
    send(swap5, got5, s_send.at[5], s_recv.at[5], rep=other)
    drain(got5, s_recv.at[5])
    first = jnp.where(r == 0, swap5[...], got5[...])
    second = jnp.where(r == 0, got5[...], swap5[...])
    slot_here = k_here * blocks + g_here
    ag5[slot_here] = jnp.where(line < qn, first, pltpu.roll(second, qn, 0)).astype(BF16)
    across_runs(lambda g: ag5.at[slot_here], ag5.at[slot_here], 6)
    bulk(1, cuts[2], cuts[3])
    drain(ag5.at[pl.ds(0, blocks - 1)], s_recv.at[6])
    mates(lambda k: of_class(ag5, k_here), of_class(ag5, k_here), 7)
    bulk(1, cuts[1], cuts[2])
    for load in loads[9:]:
        load.wait()
    put_in_order(2)
    drain(ag5.at[pl.ds(0, (near - 1) * blocks)], s_recv.at[7])

    wide[...] = ag5[...].astype(F32)
    acc = across(wide[:, 0, :].astype(BF16), wo[:, 0:HD])
    for g in range(1, n_rep * qn):
        acc = acc + across(wide[:, g, :].astype(BF16), wo[:, g * HD : (g + 1) * HD])
    pad = jnp.zeros((rows, HD - acc.shape[1]), F32)
    part6[h] = jnp.concatenate([acc, pad], axis=1)
    for t in range(1, n_head):
        peer = lax.rem(h + t, n_head)
        send(part6.at[h], part6.at[h], s_send.at[8], s_recv.at[8], head=peer)
    drain(part6.at[pl.ds(0, n_head - 1)], s_recv.at[8])
    proj = part6[0]
    for s in range(1, n_head):
        proj = proj + part6[s]
    middle = x + proj[:, : x.shape[1]]

    square = jnp.broadcast_to(jnp.sum(middle * middle, axis=1, keepdims=True), (rows, HD))
    y = both_parts(middle * fgain[...])
    fn = wg.shape[1] // n_rep // HD
    pg, pu = (folded(dot(y, w[...])) for w in (wg, wu))
    for side, buf in ((1, far7), (0, own7)):
        here = (r == 0) if side == 0 else (r != 0)
        for p, start in ((pg, 0), (pu, 8)):
            for c in range(fn):
                buf[:, start + c, :] = jnp.where(
                    here, p[:, c * HD : (c + 1) * HD], p[:, (fn + c) * HD : (fn + c + 1) * HD]
                )
            for c in range(fn, 8):
                buf[:, start + c, :] = square
        if side == 1:
            send(far7, got7, s_send.at[9], s_recv.at[9], rep=other)
    drain(got7, s_recv.at[9])
    own7[...] = own7[...] + got7[...]
    mates(lambda k: of_class(own7, k), near8.at[k_here], 10)
    near8[k_here] = own7[pl.ds(k_here * blocks, blocks)]
    bulk(1, cuts[0], cuts[1])
    drain(near8.at[pl.ds(0, near - 1)], s_recv.at[10])
    total = jnp.sum(near8[...], axis=0)
    square = total[:, 7, :]
    near8[0] = total
    near8[0, :, 15, :] = square - square.astype(BF16).astype(F32)
    part8[...] = near8[0].astype(BF16)
    across_runs(lambda g: part8.at[g], row8.at[g_here], 11)
    row8[g_here] = part8[g_here]
    bulk(2, cuts[2], cuts[3])
    put_in_order(3)

    drain(row8.at[pl.ds(0, blocks - 1)], s_recv.at[11])
    total = jnp.sum(row8[...].astype(F32), axis=0)
    scale = lax.rsqrt((total[7:8, 0:1] + total[15:16, 0:1]) / D + EPSILON)
    gate = total[0:8] * scale
    up = total[8:16] * scale
    hidden = gate / (1.0 + jnp.exp(-gate)) * up
    ag9[slot_here] = jnp.where(line < fn, hidden, 0.0).astype(BF16)
    across_runs(lambda g: ag9.at[slot_here], ag9.at[slot_here], 12)
    bulk(2, cuts[1], cuts[2])
    drain(ag9.at[pl.ds(0, blocks - 1)], s_recv.at[12])
    mates(lambda k: of_class(ag9, k_here), of_class(ag9, k_here), 13)
    bulk(2, cuts[0], cuts[1])
    bulk(3, 1, reach)
    drain(ag9.at[pl.ds(0, (near - 1) * blocks)], s_recv.at[13])
    send(ag9, pair9, s_send.at[14], s_recv.at[14], rep=other)

    def down(ref, which):
        wide[...] = ref[...].astype(F32)
        acc = jnp.zeros((rows, x.shape[1]), F32)
        for c in range(fn):
            start = pl.multiple_of((which * fn + c) * HD, HD)
            acc = acc + across(wide[:, c, :].astype(BF16), wd[:, pl.ds(start, HD)])
        return acc

    acc = down(ag9, r)
    drain(pair9, s_recv.at[14])
    acc = acc + down(pair9, other)
    part11[h] = jnp.concatenate([acc, pad], axis=1)
    for t in range(1, n_head):
        peer = lax.rem(h + t, n_head)
        send(part11.at[h], part11.at[h], s_send.at[15], s_recv.at[15], head=peer)
    drain(part11.at[pl.ds(0, n_head - 1)], s_recv.at[15])
    proj = part11[0]
    for s in range(1, n_head):
        proj = proj + part11[s]
    layer = (middle + proj[:, : x.shape[1]]).astype(BF16)
    layer_out[...] = lax.dot_general(
        to_row, layer, (((0,), (0,)), ((), ())), preferred_element_type=F32
    ).astype(BF16)

    for q in range(count):
        start = (q % pieces) * some
        here = z * BLK + r * half + start + lax.broadcasted_iota(jnp.int32, (some, width), 0)
        drain(arrived[q].at[pl.ds(0, n_seq - 1)], b_recv.at[q])

        def place(i, _):
            found = arrived[q][prow[i]]
            decoded[q // pieces, i, start : start + some, :] = jnp.where(
                here < lens[i], found, jnp.zeros((), found.dtype)
            )
            return 0

        lax.fori_loop(0, rows, place, 0)

    for q in range(count):
        drain(pool[q].at[pl.ds(0, (n_head - 1) * slots)], b_xsend.at[q])
        drain(ordered[q].at[pl.ds(0, n_seq - 1)], b_send.at[q])
    drain(far1, s_send.at[0])
    drain(near1.at[pl.ds(0, near - 1)], s_send.at[1])
    drain(row1.at[pl.ds(0, blocks - 1)], s_send.at[2])
    drain(tile3.at[pl.ds(0, n_kv - 1)], s_send.at[3])
    drain(state4.at[pl.ds(0, n_kv - 1)], s_send.at[4])
    drain(swap5, s_send.at[5])
    drain(ag5.at[pl.ds(0, blocks - 1)], s_send.at[6])
    drain(ag5.at[pl.ds(0, (near - 1) * blocks)], s_send.at[7])
    drain(part6.at[pl.ds(0, n_head - 1)], s_send.at[8])
    drain(far7, s_send.at[9])
    drain(near8.at[pl.ds(0, near - 1)], s_send.at[10])
    drain(row8.at[pl.ds(0, blocks - 1)], s_send.at[11])
    drain(ag9.at[pl.ds(0, blocks - 1)], s_send.at[12])
    drain(ag9.at[pl.ds(0, (near - 1) * blocks)], s_send.at[13])
    drain(ag9, s_send.at[14])
    drain(part11.at[pl.ds(0, n_head - 1)], s_send.at[15])


def shards(
    tokens,
    attn_gain,
    ffn_gain,
    w_query,
    w_key,
    w_value,
    w_out,
    w_gate,
    w_up,
    w_down,
    kv_pool,
    lengths,
    pool_row,
    block_table,
):
    rows, features = tokens.shape
    n_seq, n_head, n_rep = (lax.axis_size(a) for a in ("seq", "head", "rep"))
    slots, half = kv_pool.shape[2:4]
    width = kv_pool.shape[4] // n_head
    n_kv = n_head * n_rep

    position = jnp.sum(jnp.where(pool_row == lax.axis_index("seq"), lengths, 0)).astype(F32)
    freq_table = jnp.exp(jnp.arange(HD // 2, dtype=F32) * (-2.0 * ROPE_LOG / HD))
    angles = position * freq_table
    sine = jnp.sin(angles)
    cosine = jnp.cos(angles)
    turn = jnp.stack([jnp.concatenate([cosine, cosine]), jnp.concatenate([-sine, sine])])

    given = (
        tokens,
        pool_row[None, :],
        attn_gain[None, :],
        ffn_gain[None, :],
        turn,
        w_query,
        w_key,
        w_value,
        kv_pool,
        w_out.T,
        w_gate,
        w_up,
        w_down.T,
    )
    vmem = pl.BlockSpec(memory_space=pltpu.VMEM)
    smem = pl.BlockSpec(memory_space=pltpu.SMEM)
    pieces, near = 2, 4
    blocks = n_seq // near
    pool = (n_head * slots, half // pieces, width)
    ring = (n_seq, half // pieces, width)
    line, lines = (rows, 8, HD), (rows, 16, HD)
    return pl.pallas_call(
        functools.partial(kernel, n_seq, n_head, n_rep, near, pieces),
        out_shape=(
            jax.ShapeDtypeStruct((rows, features), BF16),
            jax.ShapeDtypeStruct((2, rows, half, width), BF16),
        ),
        in_specs=[pl.BlockSpec(memory_space=pl.ANY)] * len(given) + [smem] * 3,
        out_specs=(vmem, vmem),
        scratch_shapes=[
            *(pltpu.VMEM(a.shape, a.dtype) for a in given[:8]),
            pltpu.VMEM((2, *kv_pool.shape[2:]), BF16),
            *(pltpu.VMEM(a.shape, a.dtype) for a in given[9:]),
            *(pltpu.VMEM(pool, BF16) for _ in range(2 * pieces)),
            *(pltpu.VMEM(ring, BF16) for _ in range(4 * pieces)),
            *(pltpu.VMEM(line, F32) for _ in range(3)),
            pltpu.VMEM((near, blocks, 8, HD), F32),
            pltpu.VMEM((blocks, 8, HD), F32),
            pltpu.VMEM((blocks, 8, HD), F32),
            pltpu.VMEM((n_kv, 8, HD), F32),
            pltpu.VMEM((n_kv, 16, HD), F32),
            pltpu.VMEM((n_kv, 16, HD), F32),
            pltpu.VMEM((8, HD), F32),
            pltpu.VMEM((8, HD), F32),
            pltpu.VMEM(line, BF16),
            pltpu.VMEM(line, F32),
            pltpu.VMEM((n_head, rows, HD), F32),
            *(pltpu.VMEM(lines, F32) for _ in range(3)),
            pltpu.VMEM((near, blocks, 16, HD), F32),
            pltpu.VMEM((blocks, 16, HD), BF16),
            pltpu.VMEM((blocks, 16, HD), BF16),
            *(pltpu.VMEM(line, BF16) for _ in range(2)),
            pltpu.VMEM((n_head, rows, HD), F32),
            pltpu.SemaphoreType.DMA((16,)),
            pltpu.SemaphoreType.DMA((16,)),
            pltpu.SemaphoreType.DMA((len(given),)),
            *(pltpu.SemaphoreType.DMA((2 * pieces,)) for _ in range(4)),
        ],
        compiler_params=pltpu.CompilerParams(
            collective_id=0, has_side_effects=True, vmem_limit_bytes=60 * 1024 * 1024
        ),
        name="decode_layer",
    )(*given, block_table, pool_row, lengths)


def solution(mesh):
    in_specs = (
        P("groups", ("seq", "rep")),
        P(("seq", "rep")),
        P(("seq", "rep")),
        P(("seq", "rep"), "head"),
        P(("seq", "rep"), "head"),
        P(("seq", "rep"), "head"),
        P("head", ("seq", "rep")),
        P(("seq", "rep"), "head"),
        P(("seq", "rep"), "head"),
        P("head", ("seq", "rep")),
        P(None, ("groups", "seq"), "head", "rep", None),
        P("groups"),
        P("groups"),
        P("groups", None),
    )
    out_specs = (P("groups", ("seq", "rep")), P(None, "groups", ("seq", "rep"), "head"))
    return jax.shard_map(shards, mesh=mesh, in_specs=in_specs, out_specs=out_specs, check_vma=False)
```

time: 312 us -> 283 us (0.907)
  the two profiles are of different devices: /device:TPU:168 before, /device:TPU:33 now
where the time goes in v3:
time: 283 us
  Pallas kernels  275 us (97%)
  local copies, waits for them, and re-layouts  4.45 us (2%)
    pallas_call x1, Pallas kernels, shards(): pl.pallas_call(functools.partial(kernel, n_seq, n_head, n_rep, near, piec...  275 us

profile of v3, /device:TPU:33, one launch (start us, length us, event | category | flops | bytes accessed | tf_op | source)
XLA Modules:
  0.0 283.1 jit_solution(10811155784359891410)
XLA Ops:
  0.6 1.3 fusion
  2.6 0.1 fusion.3
  2.6 0.1 fusion.1
  2.7 0.1 maximum_bitcast_fusion.1
  2.8 0.1 maximum_bitcast_fusion
  2.9 0.6 pad_maximum_fusion.refs_4_
  3.4 275.2 %decode_layer.1 = (bf16[32,64]{1,0:T(8,128)(2,1)}, bf16[2,32,64,256]{3,2,1,0:T(8,128)(2,1)}) custom-call(bf16[32,64]{1,0:T(8,128)(2,1)} %refs_0_.1, s32[1,32]{1,0:T(1,128)} %bitcast.11, f32[1,64]{1,0:T(1,128)} %bitcast.12, f32[1,64]{1,0:T(1,128)} %bitcast.13, f32[2,128]{1,0:T(2,128)} %pad_maximum_fusion.refs_4_, bf16[64,1024]{1,0:T(8,128)(2,1)} %refs_5_.1, ...), custom_call_target="tpu_custom_call" | custom-call | tf_op jit(solution)/shard_map/decode_layer/pallas_call | solution.py:471
  278.7 1.3 copy.18
  280.0 3.2 %copy.19 = bf16[2,32,64,256]{3,2,1,0:T(8,128)(2,1)} copy(bf16[2,32,64,256]{3,2,1,0:T(8,128)(2,1)} %get-tuple-element.7) | data formatting | bytes 4194304

commit v4 on v3

--- a/solution.py
+++ b/solution.py
@@ -3,6 +3,7 @@
 
 import jax
 import jax.numpy as jnp
+import numpy as np
 from jax import lax
 from jax.experimental import pallas as pl
 from jax.experimental.pallas import tpu as pltpu
@@ -17,6 +18,9 @@
 EPSILON = 1e-05
 ROPE_LOG = math.log(500000.0)
 FLOOR_SCORE = -1e30
+STEP = 64
+PIECES = 4
+WAVES = ((0, 1), (2,), (3,), (4,), (5,), (6,), (7,))
 MESH = pl.DeviceIdType.MESH
 BF16 = jnp.bfloat16
 F32 = jnp.float32
@@ -58,18 +62,19 @@
 
 def kernel(n_seq, n_head, n_rep, near, pieces, *refs):
     (
-        tok_h, pvec_h, again_h, fgain_h, turn_h, wq_h, wk_h, wv_h, kv_h, wo_h, wg_h, wu_h, wd_h,
+        tok_h, pvec_h, again_h, fgain_h, far_h, fine_h, wq_h, wk_h, wv_h, kv_h, wo_h, wg_h, wu_h, wd_h,
+        table_h, prow_h, lens_h,
+        layer_out, decoded,
+        tok, pvec, again, fgain, far, fine, wq, wk, wv, kv, wo, wg, wu, wd,
         table, prow, lens,
-        layer_out, decoded,
-        tok, pvec, again, fgain, turn, wq, wk, wv, kv, wo, wg, wu, wd,
-    ) = refs[:31]
+    ) = refs[:36]
     count = 2 * pieces
-    pool, ordered, arrived = (refs[31 + k * count : 31 + (k + 1) * count] for k in range(3))
+    pool, ordered, arrived = (refs[36 + k * count : 36 + (k + 1) * count] for k in range(3))
     (
         own1, far1, got1, near1, part1, row1, tile3, state4, got4, swap5, got5, ag5, wide,
         part6, own7, far7, got7, near8, part8, row8, ag9, pair9, part11,
         s_send, s_recv, s_load, b_xsend, b_xrecv, b_send, b_recv,
-    ) = refs[31 + 3 * count :]
+    ) = refs[36 + 3 * count :]
     z = lax.axis_index("seq")
     h = lax.axis_index("head")
     r = lax.axis_index("rep")
@@ -85,28 +90,13 @@
     some = half // pieces
     width = decoded.shape[3]
 
-    loads = [
-        pltpu.make_async_copy(src, dst, s_load.at[k])
-        for k, (src, dst) in enumerate(
-            zip(
-                (kv_h.at[:, 0], tok_h, pvec_h, again_h, fgain_h, turn_h, wq_h, wk_h, wv_h,
-                 wo_h, wg_h, wu_h, wd_h),
-                (kv, tok, pvec, again, fgain, turn, wq, wk, wv, wo, wg, wu, wd),
-            )
+    barrier = pltpu.get_barrier_semaphore()
+
+    for d in range(1, n_seq):
+        d = (n_seq - d + d % 2) // 2 * (1 if d % 2 else -1)
+        pl.semaphore_signal(
+            barrier, inc=1, device_id={"seq": lax.rem(z + d + n_seq, n_seq)}, device_id_type=MESH
         )
-    ]
-    for load in loads:
-        load.start()
-
-    barrier = pltpu.get_barrier_semaphore()
-
-    def greet_seq(d, _):
-        pl.semaphore_signal(
-            barrier, inc=1, device_id={"seq": lax.rem(z + d, n_seq)}, device_id_type=MESH
-        )
-        return 0
-
-    lax.fori_loop(1, n_seq, greet_seq, 0)
     for t in range(1, n_kv):
         peer = lax.rem(j + t, n_kv)
         pl.semaphore_signal(
@@ -115,6 +105,20 @@
             device_id={"head": peer // n_rep, "rep": peer % n_rep},
             device_id_type=MESH,
         )
+    loads = [
+        pltpu.make_async_copy(src, dst, s_load.at[k])
+        for k, (src, dst) in enumerate(
+            zip(
+                (kv_h.at[:, 0], tok_h, pvec_h, again_h, fgain_h, far_h, fine_h, wq_h, wk_h, wv_h,
+                 table_h, prow_h, lens_h, wo_h, wg_h, wu_h, wd_h),
+                (kv, tok, pvec, again, fgain, far, fine, wq, wk, wv,
+                 table, prow, lens, wo, wg, wu, wd),
+            )
+        )
+    ]
+    for load in loads:
+        load.start()
+
     loads[0].wait()
     pl.semaphore_wait(barrier, n_seq - 1 + n_kv - 1)
 
@@ -137,7 +141,7 @@
                 head=peer,
             )
 
-    for load in loads[1:9]:
+    for load in loads[1:13]:
         load.wait()
     at = lax.broadcasted_iota(jnp.int32, (rows, rows), 0)
     to_row = (at % blocks) * near + at // blocks == pvec[...]
@@ -216,10 +220,12 @@
 
         lax.fori_loop(lo, hi, body, 0)
 
-    cuts = (1, 1 + n_seq * 9 // 32, 1 + n_seq * 13 // 32, reach)
-
-    put_in_order(0)
-    bulk(0, 1, reach)
+    def wave(n):
+        for q in WAVES[n]:
+            put_in_order(q)
+            bulk(q, 1, reach)
+
+    wave(0)
 
     slot_of = lax.broadcasted_iota(jnp.int32, (1, held), 1) // half
     place_of = lax.broadcasted_iota(jnp.int32, (1, held), 1) % half
@@ -235,7 +241,12 @@
     scale = lax.rsqrt(total[qn + 2 : qn + 3, 0:1] / D + EPSILON)
     total = total * scale
     line = lax.broadcasted_iota(jnp.int32, (8, HD), 0)
-    turned = total * turn[0:1, :] + pltpu.roll(total, HD // 2, 1) * turn[1:2, :]
+    lane = lax.broadcasted_iota(jnp.int32, (8, HD), 1)
+    whole, part = far[length // STEP], fine[length % STEP]
+    cosine = whole[0:1] * part[0:1] - whole[1:2] * part[1:2]
+    sine = whole[1:2] * part[0:1] + whole[0:1] * part[1:2]
+    sine = jnp.where(lane < HD // 2, -sine, sine)
+    turned = total * cosine + pltpu.roll(total, HD // 2, 1) * sine
     mine = jnp.where(line <= qn, turned, jnp.where(line == qn + 1, total, 0.0))
     mine = mine.astype(BF16).astype(F32)
     tile3[j] = mine
@@ -248,7 +259,6 @@
     drain(tile3.at[pl.ds(0, n_kv - 1)], s_recv.at[3])
 
     factor = 1.0 / math.sqrt(HD)
-    lane = lax.broadcasted_iota(jnp.int32, (8, HD), 1)
     for g in range(n_kv):
         keys = kv[0, :, :, g * HD : (g + 1) * HD].reshape(held, HD)
         values = kv[1, :, :, g * HD : (g + 1) * HD].reshape(held, HD)
@@ -266,7 +276,6 @@
             head=peer // n_rep, rep=peer % n_rep,
         )
     got4[j] = state4[j]
-    put_in_order(1)
     drain(got4.at[pl.ds(0, n_kv - 1)], s_recv.at[4])
     own_score = jnp.sum(mine * mine[qn : qn + 1, :], axis=1, keepdims=True) * factor
     top = own_score
@@ -287,13 +296,12 @@
     slot_here = k_here * blocks + g_here
     ag5[slot_here] = jnp.where(line < qn, first, pltpu.roll(second, qn, 0)).astype(BF16)
     across_runs(lambda g: ag5.at[slot_here], ag5.at[slot_here], 6)
-    bulk(1, cuts[2], cuts[3])
+    wave(1)
     drain(ag5.at[pl.ds(0, blocks - 1)], s_recv.at[6])
     mates(lambda k: of_class(ag5, k_here), of_class(ag5, k_here), 7)
-    bulk(1, cuts[1], cuts[2])
-    for load in loads[9:]:
+    wave(2)
+    for load in loads[13:]:
         load.wait()
-    put_in_order(2)
     drain(ag5.at[pl.ds(0, (near - 1) * blocks)], s_recv.at[7])
 
     wide[...] = ag5[...].astype(F32)
@@ -330,7 +338,7 @@
     own7[...] = own7[...] + got7[...]
     mates(lambda k: of_class(own7, k), near8.at[k_here], 10)
     near8[k_here] = own7[pl.ds(k_here * blocks, blocks)]
-    bulk(1, cuts[0], cuts[1])
+    wave(3)
     drain(near8.at[pl.ds(0, near - 1)], s_recv.at[10])
     total = jnp.sum(near8[...], axis=0)
     square = total[:, 7, :]
@@ -339,8 +347,7 @@
     part8[...] = near8[0].astype(BF16)
     across_runs(lambda g: part8.at[g], row8.at[g_here], 11)
     row8[g_here] = part8[g_here]
-    bulk(2, cuts[2], cuts[3])
-    put_in_order(3)
+    wave(4)
 
     drain(row8.at[pl.ds(0, blocks - 1)], s_recv.at[11])
     total = jnp.sum(row8[...].astype(F32), axis=0)
@@ -350,11 +357,10 @@
     hidden = gate / (1.0 + jnp.exp(-gate)) * up
     ag9[slot_here] = jnp.where(line < fn, hidden, 0.0).astype(BF16)
     across_runs(lambda g: ag9.at[slot_here], ag9.at[slot_here], 12)
-    bulk(2, cuts[1], cuts[2])
+    wave(5)
     drain(ag9.at[pl.ds(0, blocks - 1)], s_recv.at[12])
     mates(lambda k: of_class(ag9, k_here), of_class(ag9, k_here), 13)
-    bulk(2, cuts[0], cuts[1])
-    bulk(3, 1, reach)
+    wave(6)
     drain(ag9.at[pl.ds(0, (near - 1) * blocks)], s_recv.at[13])
     send(ag9, pair9, s_send.at[14], s_recv.at[14], rep=other)
 
@@ -415,6 +421,12 @@
     drain(ag9.at[pl.ds(0, (near - 1) * blocks)], s_send.at[13])
     drain(ag9, s_send.at[14])
     drain(part11.at[pl.ds(0, n_head - 1)], s_send.at[15])
+
+
+def angle_table(positions):
+    turns = np.exp(np.arange(HD // 2) * (-2.0 * ROPE_LOG / HD))
+    angles = positions[:, None] * np.concatenate([turns, turns])[None, :]
+    return jnp.asarray(np.stack([np.cos(angles), np.sin(angles)], axis=1), F32)
 
 
 def shards(
@@ -439,19 +451,13 @@
     width = kv_pool.shape[4] // n_head
     n_kv = n_head * n_rep
 
-    position = jnp.sum(jnp.where(pool_row == lax.axis_index("seq"), lengths, 0)).astype(F32)
-    freq_table = jnp.exp(jnp.arange(HD // 2, dtype=F32) * (-2.0 * ROPE_LOG / HD))
-    angles = position * freq_table
-    sine = jnp.sin(angles)
-    cosine = jnp.cos(angles)
-    turn = jnp.stack([jnp.concatenate([cosine, cosine]), jnp.concatenate([-sine, sine])])
-
     given = (
         tokens,
         pool_row[None, :],
         attn_gain[None, :],
         ffn_gain[None, :],
-        turn,
+        angle_table(np.arange(BLK * block_table.shape[1] // STEP + 1) * STEP),
+        angle_table(np.arange(STEP)),
         w_query,
         w_key,
         w_value,
@@ -460,10 +466,13 @@
         w_gate,
         w_up,
         w_down.T,
+        block_table,
+        pool_row,
+        lengths,
     )
     vmem = pl.BlockSpec(memory_space=pltpu.VMEM)
-    smem = pl.BlockSpec(memory_space=pltpu.SMEM)
-    pieces, near = 2, 4
+    hbm = pl.BlockSpec(memory_space=pltpu.HBM)
+    pieces, near = PIECES, 4
     blocks = n_seq // near
     pool = (n_head * slots, half // pieces, width)
     ring = (n_seq, half // pieces, width)
@@ -474,12 +483,13 @@
             jax.ShapeDtypeStruct((rows, features), BF16),
             jax.ShapeDtypeStruct((2, rows, half, width), BF16),
         ),
-        in_specs=[pl.BlockSpec(memory_space=pl.ANY)] * len(given) + [smem] * 3,
+        in_specs=[hbm] * len(given),
         out_specs=(vmem, vmem),
         scratch_shapes=[
-            *(pltpu.VMEM(a.shape, a.dtype) for a in given[:8]),
+            *(pltpu.VMEM(a.shape, a.dtype) for a in given[:9]),
             pltpu.VMEM((2, *kv_pool.shape[2:]), BF16),
-            *(pltpu.VMEM(a.shape, a.dtype) for a in given[9:]),
+            *(pltpu.VMEM(a.shape, a.dtype) for a in given[10:14]),
+            *(pltpu.SMEM(a.shape, a.dtype) for a in given[14:]),
             *(pltpu.VMEM(pool, BF16) for _ in range(2 * pieces)),
             *(pltpu.VMEM(ring, BF16) for _ in range(4 * pieces)),
             *(pltpu.VMEM(line, F32) for _ in range(3)),
@@ -506,10 +516,10 @@
             *(pltpu.SemaphoreType.DMA((2 * pieces,)) for _ in range(4)),
         ],
         compiler_params=pltpu.CompilerParams(
-            collective_id=0, has_side_effects=True, vmem_limit_bytes=60 * 1024 * 1024
+            collective_id=0, has_side_effects=True, vmem_limit_bytes=40 * 1024 * 1024
         ),
         name="decode_layer",
-    )(*given, block_table, pool_row, lengths)
+    )(*(pltpu.with_memory_space_constraint(a, pltpu.HBM) for a in given))
 
 
 def solution(mesh):

time: 283 us -> 267 us (0.943)
  Pallas kernels: 275 us -> 263 us
    pallas_call x1, Pallas kernels: 275 us -> 263 us  [shards(): pl.pallas_call(functools.partial(kernel, n_seq, n_head, n_rep, near, piec...]
where the time goes in v4:
time: 267 us; the launch traced here: 266 us
  Pallas kernels  263 us (99%)
    pallas_call x1, Pallas kernels, shards(): pl.pallas_call(functools.partial(kernel, n_seq, n_head, n_rep, near, piec...  263 us

profile of v4, /device:TPU:33, one launch (start us, length us, event | category | flops | bytes accessed | tf_op | source)
XLA Modules:
  0.0 265.8 jit_solution(6377411739888177952)
XLA Ops:
  0.6 263.3 %decode_layer.1 = (bf16[32,64]{1,0:T(8,128)(2,1)S(1)}, bf16[2,32,64,256]{3,2,1,0:T(8,128)(2,1)S(1)}) custom-call(bf16[32,64]{1,0:T(8,128)(2,1)} %refs_0_.1, s32[1,32]{1,0:T(1,128)} %bitcast.7, f32[1,64]{1,0:T(1,128)} %bitcast.8, f32[1,64]{1,0:T(1,128)} %bitcast.9, f32[65,2,128]{2,1,0:T(2,128)} %constant.4.clone.refs_4_, ...), custom_call_target="tpu_custom_call" | custom-call | tf_op jit(solution)/shard_map/decode_layer/pallas_call | solution.py:480
  263.9 0.6 copy.20
  264.5 1.3 copy.21

commit v5 on v4

--- a/solution.py
+++ b/solution.py
@@ -72,8 +72,8 @@
     pool, ordered, arrived = (refs[36 + k * count : 36 + (k + 1) * count] for k in range(3))
     (
         own1, far1, got1, near1, part1, row1, tile3, state4, got4, swap5, got5, ag5, wide,
-        part6, own7, far7, got7, near8, part8, row8, ag9, pair9, part11,
-        s_send, s_recv, s_load, b_xsend, b_xrecv, b_send, b_recv,
+        part6, own7, far7, got7, out8, near8, sum8, part8, row8, ag9, pair9, part11,
+        s_send, s_recv, s_load, b_xsend, b_xrecv, b_send, b_recv, s_ready,
     ) = refs[36 + 3 * count :]
     z = lax.axis_index("seq")
     h = lax.axis_index("head")
@@ -92,8 +92,7 @@
 
     barrier = pltpu.get_barrier_semaphore()
 
-    for d in range(1, n_seq):
-        d = (n_seq - d + d % 2) // 2 * (1 if d % 2 else -1)
+    for d in (*range(1, near + 1), *range(-near, 0)):
         pl.semaphore_signal(
             barrier, inc=1, device_id={"seq": lax.rem(z + d + n_seq, n_seq)}, device_id_type=MESH
         )
@@ -120,7 +119,15 @@
         load.start()
 
     loads[0].wait()
-    pl.semaphore_wait(barrier, n_seq - 1 + n_kv - 1)
+    pl.semaphore_wait(barrier, 2 * near + n_kv - 1)
+
+    def widen(step, n):
+        for d in (step, n_seq - step):
+            pl.semaphore_signal(
+                s_ready.at[n], inc=1, device_id={"seq": lax.rem(z + d, n_seq)}, device_id_type=MESH
+            )
+
+    widen(near, 0)
 
     def columns(q, owner):
         return (
@@ -181,12 +188,17 @@
     def of_class(ref, k):
         return ref.at[pl.ds(k * blocks, blocks)]
 
+    rounds = s_ready.shape[0]
+    for n in range(1, rounds):
+        pl.semaphore_wait(s_ready.at[n - 1], 2)
+        widen(near << n, n)
     drain(got1, s_recv.at[0])
     own1[...] = own1[...] + got1[...]
     mates(lambda k: of_class(own1, k), near1.at[k_here], 1)
     near1[k_here] = own1[pl.ds(k_here * blocks, blocks)]
     drain(near1.at[pl.ds(0, near - 1)], s_recv.at[1])
     part1[...] = jnp.sum(near1[...], axis=0)
+    pl.semaphore_wait(s_ready.at[rounds - 1], 2)
     across_runs(lambda g: part1.at[g], row1.at[g_here], 2)
     row1[g_here] = part1[g_here]
 
@@ -208,6 +220,7 @@
 
     def bulk(q, lo, hi):
         def body(d, _):
+            d = hi - 1 - d
             peer = lax.rem(z + d, n_seq)
             send(ordered[q].at[peer], arrived[q].at[z], b_send.at[q], b_recv.at[q], seq=peer)
             back = lax.rem(z + n_seq - d, n_seq)
@@ -218,7 +231,7 @@
 
             return 0
 
-        lax.fori_loop(lo, hi, body, 0)
+        lax.fori_loop(0, hi - lo, body, 0)
 
     def wave(n):
         for q in WAVES[n]:
@@ -336,15 +349,18 @@
             send(far7, got7, s_send.at[9], s_recv.at[9], rep=other)
     drain(got7, s_recv.at[9])
     own7[...] = own7[...] + got7[...]
-    mates(lambda k: of_class(own7, k), near8.at[k_here], 10)
-    near8[k_here] = own7[pl.ds(k_here * blocks, blocks)]
+    square = own7[:, 7, :]
+    own7[:, 15, :] = square - square.astype(BF16).astype(F32)
+    out8[...] = own7[...].astype(BF16)
+    mates(lambda k: of_class(out8, k), near8.at[k_here], 10)
+    near8[k_here] = out8[pl.ds(k_here * blocks, blocks)]
     wave(3)
     drain(near8.at[pl.ds(0, near - 1)], s_recv.at[10])
-    total = jnp.sum(near8[...], axis=0)
-    square = total[:, 7, :]
-    near8[0] = total
-    near8[0, :, 15, :] = square - square.astype(BF16).astype(F32)
-    part8[...] = near8[0].astype(BF16)
+    sum8[...] = jnp.sum(near8[...].astype(F32), axis=0)
+    square = sum8[:, 7, :] + sum8[:, 15, :]
+    sum8[:, 7, :] = square
+    sum8[:, 15, :] = square - square.astype(BF16).astype(F32)
+    part8[...] = sum8[...].astype(BF16)
     across_runs(lambda g: part8.at[g], row8.at[g_here], 11)
     row8[g_here] = part8[g_here]
     wave(4)
@@ -473,6 +489,7 @@
     vmem = pl.BlockSpec(memory_space=pltpu.VMEM)
     hbm = pl.BlockSpec(memory_space=pltpu.HBM)
     pieces, near = PIECES, 4
+    rounds = (n_seq // (2 * near)).bit_length() - 1
     blocks = n_seq // near
     pool = (n_head * slots, half // pieces, width)
     ring = (n_seq, half // pieces, width)
@@ -505,7 +522,9 @@
             pltpu.VMEM(line, F32),
             pltpu.VMEM((n_head, rows, HD), F32),
             *(pltpu.VMEM(lines, F32) for _ in range(3)),
-            pltpu.VMEM((near, blocks, 16, HD), F32),
+            pltpu.VMEM(lines, BF16),
+            pltpu.VMEM((near, blocks, 16, HD), BF16),
+            pltpu.VMEM((blocks, 16, HD), F32),
             pltpu.VMEM((blocks, 16, HD), BF16),
             pltpu.VMEM((blocks, 16, HD), BF16),
             *(pltpu.VMEM(line, BF16) for _ in range(2)),
@@ -514,6 +533,7 @@
             pltpu.SemaphoreType.DMA((16,)),
             pltpu.SemaphoreType.DMA((len(given),)),
             *(pltpu.SemaphoreType.DMA((2 * pieces,)) for _ in range(4)),
+            pltpu.SemaphoreType.REGULAR((rounds,)),
         ],
         compiler_params=pltpu.CompilerParams(
             collective_id=0, has_side_effects=True, vmem_limit_bytes=40 * 1024 * 1024

time: 267 us -> 255 us (0.955)
  Pallas kernels: 263 us -> 252 us
    pallas_call x1, Pallas kernels: 263 us -> 252 us  [shards(): pl.pallas_call(functools.partial(kernel, n_seq, n_head, n_rep, near, piec...]
where the time goes in v5:
time: 255 us
  Pallas kernels  252 us (99%)
    pallas_call x1, Pallas kernels, shards(): pl.pallas_call(functools.partial(kernel, n_seq, n_head, n_rep, near, piec...  252 us

profile of v5, /device:TPU:33, one launch (start us, length us, event | category | flops | bytes accessed | tf_op | source)
XLA Modules:
  0.0 254.5 jit_solution(5909242077455020507)
XLA Ops:
  0.6 252.0 %decode_layer.1 = (bf16[32,64]{1,0:T(8,128)(2,1)S(1)}, bf16[2,32,64,256]{3,2,1,0:T(8,128)(2,1)S(1)}) custom-call(bf16[32,64]{1,0:T(8,128)(2,1)} %refs_0_.1, s32[1,32]{1,0:T(1,128)} %bitcast.7, f32[1,64]{1,0:T(1,128)} %bitcast.8, f32[1,64]{1,0:T(1,128)} %bitcast.9, f32[65,2,128]{2,1,0:T(2,128)} %constant.4.clone.refs_4_, ...), custom_call_target="tpu_custom_call" | custom-call | tf_op jit(solution)/shard_map/decode_layer/pallas_call | solution.py:497
  252.6 0.6 copy.20
  253.2 1.3 copy.21

commit v6 on v5

--- a/solution.py
+++ b/solution.py
@@ -20,7 +20,7 @@
 FLOOR_SCORE = -1e30
 STEP = 64
 PIECES = 4
-WAVES = ((0, 1), (2,), (3,), (4,), (5,), (6,), (7,))
+WAVES = ((1,), (2,), (3,), (4,), (5,), (6,), (7,))
 MESH = pl.DeviceIdType.MESH
 BF16 = jnp.bfloat16
 F32 = jnp.float32
@@ -188,6 +188,9 @@
     def of_class(ref, k):
         return ref.at[pl.ds(k * blocks, blocks)]
 
+    owner = lax.fori_loop(0, rows, lambda i, at: jnp.where(prow[i] == z, i, at), 0)
+    length = lens[owner]
+
     rounds = s_ready.shape[0]
     for n in range(1, rounds):
         pl.semaphore_wait(s_ready.at[n - 1], 2)
@@ -196,14 +199,6 @@
     own1[...] = own1[...] + got1[...]
     mates(lambda k: of_class(own1, k), near1.at[k_here], 1)
     near1[k_here] = own1[pl.ds(k_here * blocks, blocks)]
-    drain(near1.at[pl.ds(0, near - 1)], s_recv.at[1])
-    part1[...] = jnp.sum(near1[...], axis=0)
-    pl.semaphore_wait(s_ready.at[rounds - 1], 2)
-    across_runs(lambda g: part1.at[g], row1.at[g_here], 2)
-    row1[g_here] = part1[g_here]
-
-    owner = lax.fori_loop(0, rows, lambda i, at: jnp.where(prow[i] == z, i, at), 0)
-    length = lens[owner]
 
     def put_in_order(q):
         pool[q][pl.ds(h * slots, slots)] = kv[columns(q, h)]
@@ -238,6 +233,16 @@
             put_in_order(q)
             bulk(q, 1, reach)
 
+    known = near << (rounds - 1)
+    put_in_order(0)
+    bulk(0, 1, known + 1)
+    drain(near1.at[pl.ds(0, near - 1)], s_recv.at[1])
+    part1[...] = jnp.sum(near1[...], axis=0)
+    pl.semaphore_wait(s_ready.at[rounds - 1], 2)
+    across_runs(lambda g: part1.at[g], row1.at[g_here], 2)
+    row1[g_here] = part1[g_here]
+
+    bulk(0, known + 1, reach)
     wave(0)
 
     slot_of = lax.broadcasted_iota(jnp.int32, (1, held), 1) // half

time: 255 us -> 253 us (level)
  no operation moved by 1% of the time
where the time goes in v6:
time: 253 us
  Pallas kernels  251 us (99%)
    pallas_call x1, Pallas kernels, shards(): pl.pallas_call(functools.partial(kernel, n_seq, n_head, n_rep, near, piec...  251 us

profile of v6, /device:TPU:33, one launch (start us, length us, event | category | flops | bytes accessed | tf_op | source)
XLA Modules:
  0.0 253.2 jit_solution(2342641085511792506)
XLA Ops:
  0.6 250.7 %decode_layer.1 = (bf16[32,64]{1,0:T(8,128)(2,1)S(1)}, bf16[2,32,64,256]{3,2,1,0:T(8,128)(2,1)S(1)}) custom-call(bf16[32,64]{1,0:T(8,128)(2,1)} %refs_0_.1, s32[1,32]{1,0:T(1,128)} %bitcast.7, f32[1,64]{1,0:T(1,128)} %bitcast.8, f32[1,64]{1,0:T(1,128)} %bitcast.9, f32[65,2,128]{2,1,0:T(2,128)} %constant.4.clone.refs_4_, ...), custom_call_target="tpu_custom_call" | custom-call | tf_op jit(solution)/shard_map/decode_layer/pallas_call | solution.py:502
  251.3 0.6 copy.20
  251.9 1.3 copy.21

commit v7 on v6

--- a/solution.py
+++ b/solution.py
@@ -20,7 +20,7 @@
 FLOOR_SCORE = -1e30
 STEP = 64
 PIECES = 4
-WAVES = ((1,), (2,), (3,), (4,), (5,), (6,), (7,))
+WAVES = (((1, 1), (2, 1)), ((3, 1),), ((4, 1),), ((5, 1),), ((6, 1),), ((7, 0),), ())
 MESH = pl.DeviceIdType.MESH
 BF16 = jnp.bfloat16
 F32 = jnp.float32
@@ -212,6 +212,7 @@
         arrived[q][z] = ordered[q][z]
 
     reach = n_seq // 2 + 1
+    known = near << (rounds - 1)
 
     def bulk(q, lo, hi):
         def body(d, _):
@@ -229,11 +230,10 @@
         lax.fori_loop(0, hi - lo, body, 0)
 
     def wave(n):
-        for q in WAVES[n]:
+        for q, near_too in WAVES[n]:
             put_in_order(q)
-            bulk(q, 1, reach)
-
-    known = near << (rounds - 1)
+            bulk(q, 1 if near_too else known + 1, reach)
+
     put_in_order(0)
     bulk(0, 1, known + 1)
     drain(near1.at[pl.ds(0, near - 1)], s_recv.at[1])
@@ -382,6 +382,7 @@
     drain(ag9.at[pl.ds(0, blocks - 1)], s_recv.at[12])
     mates(lambda k: of_class(ag9, k_here), of_class(ag9, k_here), 13)
     wave(6)
+    bulk(count - 1, 1, known + 1)
     drain(ag9.at[pl.ds(0, (near - 1) * blocks)], s_recv.at[13])
     send(ag9, pair9, s_send.at[14], s_recv.at[14], rep=other)
 

time: 253 us -> 261 us (1.032)
  Pallas kernels: 251 us -> 258 us
    pallas_call x1, Pallas kernels: 251 us -> 258 us  [shards(): pl.pallas_call(functools.partial(kernel, n_seq, n_head, n_rep, near, piec...]
where the time goes in v7:
time: 261 us
  Pallas kernels  258 us (99%)
    pallas_call x1, Pallas kernels, shards(): pl.pallas_call(functools.partial(kernel, n_seq, n_head, n_rep, near, piec...  258 us

profile of v7, /device:TPU:33, one launch (start us, length us, event | category | flops | bytes accessed | tf_op | source)
XLA Modules:
  0.0 260.5 jit_solution(969282912820727391)
XLA Ops:
  0.6 258.0 %decode_layer.1 = (bf16[32,64]{1,0:T(8,128)(2,1)S(1)}, bf16[2,32,64,256]{3,2,1,0:T(8,128)(2,1)S(1)}) custom-call(bf16[32,64]{1,0:T(8,128)(2,1)} %refs_0_.1, s32[1,32]{1,0:T(1,128)} %bitcast.7, f32[1,64]{1,0:T(1,128)} %bitcast.8, f32[1,64]{1,0:T(1,128)} %bitcast.9, f32[65,2,128]{2,1,0:T(2,128)} %constant.4.clone.refs_4_, ...), custom_call_target="tpu_custom_call" | custom-call | tf_op jit(solution)/shard_map/decode_layer/pallas_call | solution.py:503
  258.6 0.6 copy.20
  259.2 1.3 copy.21
